TPU v7x, 128 devices: a whole 4x4x4 slice. The times are simulated.
128 devices in a mesh: tm: 8 (over y, z_lo), freq: 16 (over x, z_hi, core).
Axes of the slice: x: 4, y: 4, z: 4 (z_hi: 2, z_lo: 2; z = z_hi * 2 + z_lo), core: 2. Of those that a mesh axis runs over, the one named last changes fastest.
Arguments:
- records: bfloat16 [1024, 1024, 512], P('freq', 'tm'), may hold values from -4 to 4
- gap_flags: int32 [1024, 32], P('freq', 'tm'), may hold values from -2147483648 to 2147483647
- station_mask: int32 [1024], P('freq'), may hold values 0 or 1
Outputs:
- cross_spectra: float32 [32, 2, 1024, 1024], P('freq', None, 'tm')
All inputs are finite; a program needn't handle non-finite values. No bound on the sum of `station_mask` on one device may be relied on, other than what follows from the above.
Results may differ from a plain program's by a relative error of at most 0.0013.
Values may be sent and summed in bfloat16 or wider, within the bound.
A program may use at most 128 MiB of HBM per device.

v0:
```python
import math

import jax
import jax.numpy as jnp
from jax import lax
from jax.sharding import PartitionSpec as P

BAND_DEV = 2


FLOOR = 0.25


def sent_to_all(shard, axis):
    copies = jnp.broadcast_to(shard, (lax.axis_size(axis), *shard.shape))
    return lax.all_to_all(copies, axis, split_axis=0, concat_axis=0, tiled=True)


def in_order(blocks, dim):
    blocks = jnp.moveaxis(blocks, 0, dim)
    shape = blocks.shape
    return blocks.reshape(*shape[:dim], shape[dim] * shape[dim + 1], *shape[dim + 2 :])


def gathered_copies(shard, axis, dim):
    blocks = sent_to_all(shard, axis)
    return in_order(blocks, dim)


def transform_table(length, bin_count):
    sample_ids = jnp.arange(length, dtype=jnp.int32)
    bin_ids = jnp.arange(bin_count, dtype=jnp.int32)
    phase_ids = bin_ids[:, None] * sample_ids[None, :] % length
    angles = phase_ids.astype(jnp.float32) * (2.0 * math.pi / length)
    window_taper = 0.5 - 0.5 * jnp.cos(sample_ids.astype(jnp.float32) * (2.0 * math.pi / length))
    factor = window_taper / math.sqrt(length)
    dft_table = jnp.concatenate([jnp.cos(angles) * factor, -jnp.sin(angles) * factor], axis=0)
    return dft_table.astype(jnp.bfloat16)


def unpack_flags(packed_words):
    shifts = jnp.arange(32, dtype=jnp.int32)
    bit_values = jnp.bitwise_and(
        jnp.right_shift(packed_words[:, :, None], shifts[None, None, :]), 1
    )
    return bit_values.reshape(packed_words.shape[0], packed_words.shape[1] * 32)


def whiten(records, band_bins):
    bin_count = band_bins + 4
    dft_table = transform_table(records.shape[-1], bin_count)
    spectrum = jnp.einsum("cl,swl->scw", dft_table, records, preferred_element_type=jnp.float32)
    real_part = spectrum[:, :bin_count]
    imag_part = spectrum[:, bin_count:]
    magnitude = jnp.sqrt(real_part * real_part + imag_part * imag_part)
    smooth = (
        magnitude[:, 0:band_bins]
        + magnitude[:, 1 : band_bins + 1]
        + magnitude[:, 2 : band_bins + 2]
        + magnitude[:, 3 : band_bins + 3]
        + magnitude[:, 4 : band_bins + 4]
    ) / 5.0
    factor = 1.0 / jnp.maximum(smooth, FLOOR)
    whitened = jnp.stack(
        [real_part[:, 2 : band_bins + 2] * factor, imag_part[:, 2 : band_bins + 2] * factor], axis=2
    )
    return whitened.astype(jnp.bfloat16)


def block_terms(left_side, right_side):
    count_rows, bin_count, _, win_count = left_side.shape
    right_rows = right_side.shape[0]
    direct_left = left_side.reshape(count_rows, bin_count, 2 * win_count)
    turned_left = jnp.concatenate([left_side[:, :, 1], -left_side[:, :, 0]], axis=2)
    direct_right = right_side.reshape(right_rows, bin_count, 2 * win_count)
    real_part = jnp.einsum(
        "ifx,jfx->ifj", direct_left, direct_right, preferred_element_type=jnp.float32
    )
    imag_part = jnp.einsum(
        "ifx,jfx->ifj", turned_left, direct_right, preferred_element_type=jnp.float32
    )
    return jnp.stack([real_part, imag_part], axis=2).reshape(count_rows, 2 * bin_count, right_rows)


def local(records, gap_flags, station_mask):
    freq_size = lax.axis_size("freq")
    time_size = lax.axis_size("tm")
    band_bins = BAND_DEV * freq_size
    whitened = whiten(records, band_bins)
    kept_words = gap_flags * station_mask[:, None]
    spectra = lax.all_to_all(whitened, "freq", split_axis=1, concat_axis=0, tiled=True)
    all_words = gathered_copies(kept_words, "freq", 0)
    here_flags = unpack_flags(all_words).astype(jnp.bfloat16)
    masked = spectra * here_flags[:, None, None, :]
    stations = spectra.shape[0]
    row_count = stations // time_size
    row_start = lax.axis_index("tm") * row_count
    every_words = gathered_copies(all_words, "tm", 1)
    every_flags = unpack_flags(every_words).astype(jnp.bfloat16)
    row_flags = lax.dynamic_slice_in_dim(every_flags, row_start, row_count, 0)
    counts = jnp.dot(row_flags, every_flags.T, preferred_element_type=jnp.float32)
    window_part = lax.all_gather(masked, "tm", axis=3, tiled=True)
    left_side = lax.dynamic_slice_in_dim(window_part, row_start, row_count, 0)
    stacks = block_terms(left_side, window_part)
    divisor = jnp.maximum(counts, 1.0)
    result = stacks / divisor[:, None, :]
    return result.reshape(row_count, BAND_DEV, 2, stations).transpose(1, 2, 0, 3)


def solution(mesh):
    placed = (P("freq", "tm", None), P("freq", "tm"), P("freq"))
    return jax.shard_map(
        local, mesh=mesh, in_specs=placed, out_specs=P("freq", None, "tm", None), check_vma=False
    )
```

profile of v0, /device:TPU:0, one launch (start us, length us, event | category | flops | bytes accessed | tf_op | source)
XLA Modules:
  0.0 248.1 jit_solution(3939052716398983114)
XLA Ops:
  6.5 0.7 broadcast_multiply_fusion
  7.2 0.7 reshape.52
  7.9 7.8 %all-to-all-start.1 = ((s32[16,1,256]{2,1,0:T(1,128)}), s32[16,1,256]{2,1,0:T(1,128)S(1)}, u32[]{:S(2)}, u32[]{:S(2)}) async-start(s32[16,1,256]{2,1,0:T(1,128)} %reshape.52), calls=%async_computation.1 | async-start | bytes 32768 | tf_op jit(solution)/shard_map/all_to_all | solution.py:16
  15.8 0.3 multiply_convert_fusion.1
  16.2 6.0 %convolution_bitcast_fusion = f32[64,72,128]{2,1,0:T(8,128)S(1)} fusion(bf16[64,128,512]{2,1,0:T(8,128)(2,1)} %param.3, bf16[36,512]{1,0:T(8,128)(2,1)S(1)} %get-tuple-element.10, bf16[36,512]{1,0:T(8,128)(2,1)S(1)} %get-tuple-element.9), kind=kOutput, calls=%fused_computation.5 | convolution fusion | flops 604127232 | bytes 10821632 | tf_op jit(solution)/shard_map/cl,swl->scw/dot_general | solution.py:52
  22.2 0.5 fusion.4
  22.7 0.7 fusion.13
  23.4 0.2 fusion.14
  23.6 0.1 pad_maximum_fusion
  23.7 1.4 copy.23
  25.1 7.2 %all-to-all-start = ((bf16[64,32,2,128]{3,0,2,1:T(8,128)(2,1)}), bf16[64,32,2,128]{3,0,2,1:T(8,128)(2,1)S(1)}, u32[]{:S(2)}, u32[]{:S(2)}) async-start(bf16[64,32,2,128]{3,0,2,1:T(8,128)(2,1)} %copy.23), calls=%async_computation | async-start | bytes 2097152 | tf_op jit(solution)/shard_map/all_to_all | solution.py:91
  32.4 0.5 broadcast.56
  33.0 0.6 reduce
  33.7 0.1 fusion.17
  33.9 0.2 copy.26
  34.1 16.2 %all-to-all-done = bf16[64,32,2,128]{3,0,2,1:T(8,128)(2,1)S(1)} async-done(((bf16[64,32,2,128]{3,0,2,1:T(8,128)(2,1)}), bf16[64,32,2,128]{3,0,2,1:T(8,128)(2,1)S(1)}, u32[]{:S(2)}, u32[]{:S(2)}) %all-to-all-start) | async-done | bytes 1048608 | tf_op jit(solution)/shard_map/all_to_all | solution.py:91
  50.3 1.1 bitcast_multiply_fusion
  51.5 0.7 broadcast_in_dim.5
  52.2 4.9 %all-to-all-start.2 = ((s32[8,1024,4]{1,2,0:T(4,128)}), s32[8,1024,4]{1,2,0:T(4,128)S(1)}, u32[]{:S(2)}, u32[]{:S(2)}) async-start(s32[8,1024,4]{1,2,0:T(4,128)} %broadcast_in_dim.5), calls=%async_computation.2 | async-start | bytes 262144 | tf_op jit(solution)/shard_map/all_to_all | solution.py:16
  57.2 6.8 %all-to-all-done.2 = s32[8,1024,4]{1,2,0:T(4,128)S(1)} async-done(((s32[8,1024,4]{1,2,0:T(4,128)}), s32[8,1024,4]{1,2,0:T(4,128)S(1)}, u32[]{:S(2)}, u32[]{:S(2)}) %all-to-all-start.2) | async-done | bytes 131104 | tf_op jit(solution)/shard_map/all_to_all | solution.py:16
  64.1 0.5 fusion.1
  64.6 0.5 convolution_maximum_fusion
  65.1 0.2 copy.29
  65.3 154.7 %all-gather.2.cloned.1.call-done = bf16[1024,2,2,1024]{3,0,1,2:T(8,128)(2,1)} async-done(((bf16[1024,2,2,128]{3,0,1,2:T(8,128)(2,1)}), bf16[1024,2,2,1024]{3,0,1,2:T(8,128)(2,1)}) %all-gather.2.cloned.1.call-update) | async-done | bytes 8388624 | tf_op jit(solution)/shard_map/all_gather | solution.py:102
  220.1 8.1 %copy.31 = bf16[2,2,128,8,1024]{4,3,0,2,1:T(8,128)(2,1)} copy(bf16[2,2,128,8,1024]{4,3,2,1,0:T(8,128)(2,1)} %bitcast.62) | data formatting | bytes 16777216 | tf_op jit(solution)/shard_map/reshape | solution.py:75
  228.1 1.4 dynamic-slice_bitcast_fusion
  229.6 0.1 copy.32
  229.7 5.9 %convolution_bitcast_fusion.2 = f32[128,2,1,1024]{0,3,1,2:T(8,128)S(1)} fusion(bf16[1024,2,2048]{2,0,1:T(8,128)(2,1)} %bitcast.58, bf16[128,2,2048]{2,0,1:T(8,128)(2,1)S(1)} %bitcast.63), kind=kOutput, calls=%fused_computation.7 | convolution fusion | flops 1073741824 | bytes 10485760 | tf_op jit(solution)/shard_map/ifx,jfx->ifj/dot_general | solution.py:76
  235.5 1.3 dynamic-slice_bitcast_fusion.1
  236.9 2.3 convolution_bitcast_fusion.1
  239.3 0.2 fusion.2
  239.5 1.8 copy.30
  (19 shorter events, 0.6 us)
Async XLA Ops:
  7.9 17.1 %all-to-all-start.1 = ((s32[16,1,256]{2,1,0:T(1,128)}), s32[16,1,256]{2,1,0:T(1,128)S(1)}, u32[]{:S(2)}, u32[]{:S(2)}) async-start(s32[16,1,256]{2,1,0:T(1,128)} %reshape.52), calls=%async_computation.1 | async-start | bytes 32768 | tf_op jit(solution)/shard_map/all_to_all | solution.py:16
  25.1 25.2 %all-to-all-start = ((bf16[64,32,2,128]{3,0,2,1:T(8,128)(2,1)}), bf16[64,32,2,128]{3,0,2,1:T(8,128)(2,1)S(1)}, u32[]{:S(2)}, u32[]{:S(2)}) async-start(bf16[64,32,2,128]{3,0,2,1:T(8,128)(2,1)} %copy.23), calls=%async_computation | async-start | bytes 2097152 | tf_op jit(solution)/shard_map/all_to_all | solution.py:91
  32.3 187.8 %all-gather.2.cloned.1.call-start = ((), (), s32[]{:S(2)}) async-start(), calls=%async_computation.3 | async-start | bytes 9437184 | tf_op jit(solution)/shard_map/all_gather | solution.py:102
  52.2 11.9 %all-to-all-start.2 = ((s32[8,1024,4]{1,2,0:T(4,128)}), s32[8,1024,4]{1,2,0:T(4,128)S(1)}, u32[]{:S(2)}, u32[]{:S(2)}) async-start(s32[8,1024,4]{1,2,0:T(4,128)} %broadcast_in_dim.5), calls=%async_computation.2 | async-start | bytes 262144 | tf_op jit(solution)/shard_map/all_to_all | solution.py:16
  228.1 8.8 %slice-start = ((s8[8388608]{0:T(1024)(128)(4,1)}), s8[4194304]{0:T(1024)(128)(4,1)S(1)}, s32[]{:S(2)}) async-start(s8[8388608]{0:T(1024)(128)(4,1)} %bitcast.59), calls=%async_computation.4 | async-start | bytes 8388608
  229.7 7.2 %slice-start.1 = ((s8[8388608]{0:T(1024)(128)(4,1)}), s8[4194304]{0:T(1024)(128)(4,1)S(1)}, s32[]{:S(2)}) async-start(s8[8388608]{0:T(1024)(128)(4,1)} %bitcast.59), calls=%async_computation.5 | async-start | bytes 8388608
Sparse Core Ops, SparseCore 0:
  51.6 168.3 all-gather.1
where the time goes:
time: 249 us; the launch traced here: 248 us
  waiting for transfers between devices  178 us (71%)
  starting transfers between devices  20 us (8%)
  local copies, waits for them, and re-layouts  15.5 us (6%)
  matrix products  14.7 us (6%)
  between operations  13.6 us (5%)
  other arithmetic  6.52 us (3%)
    all_gather x1, waiting for transfers between devices, local(): window_part = lax.all_gather(masked, 'tm', axis=3, tiled=True)  155 us
    all_to_all x1, waiting for transfers between devices, local(): lax.all_to_all(whitened, 'freq', split_axis=1, concat_axis=0, tiled=True)  16.2 us
    all_to_all x2, starting transfers between devices, sent_to_all(): return lax.all_to_all(copies, axis, split_axis=0, concat_axis=0, tiled=True)  12.8 us
    reshape x1, local copies, waits for them, and re-layouts, block_terms(): direct_right = right_side.reshape(right_rows, bin_count, 2 * win_count)  8.06 us
    all_to_all x1, starting transfers between devices, local(): lax.all_to_all(whitened, 'freq', split_axis=1, concat_axis=0, tiled=True)  7.22 us
    all_to_all x2, waiting for transfers between devices, sent_to_all(): return lax.all_to_all(copies, axis, split_axis=0, concat_axis=0, tiled=True)  6.85 us
    dot_general x1, matrix products, whiten(): jnp.einsum('cl,swl->scw', dft_table, records, preferred_element_type=jnp....  6.01 us
    dot_general x1, matrix products, block_terms(): jnp.einsum('ifx,jfx->ifj', direct_left, direct_right, preferred_element_t...  5.86 us
  transfers between devices with their start and end apart: 4, of which 3 were waited for; matrix products, arithmetic and copies ran while one was open for 5% of the time, Pallas kernels for 0%

commit v1 on v0

v1 whole, which is shorter than its diff:
```python
import math

import jax
import jax.numpy as jnp
from jax import lax
from jax.experimental import pallas as pl
from jax.experimental.pallas import tpu as pltpu
from jax.sharding import PartitionSpec as P

FLOOR = 0.25
MESH = pl.DeviceIdType.MESH
Y = 4
PLANE = 32
STA = 64
ROWS = 256
UP = (("own", 1), ("own", 2), ("fwd", 2), ("own", 0), ("fwd", 1), ("own", 3))
DOWN = (("own", 3), ("own", 0), ("fwd", 3), ("own", 2), ("own", 1), ("fwd", 0))


def transform_table(length, bin_count):
    sample_ids = jnp.arange(length, dtype=jnp.int32)
    bin_ids = jnp.arange(bin_count, dtype=jnp.int32)
    phase_ids = bin_ids[:, None] * sample_ids[None, :] % length
    angles = phase_ids.astype(jnp.float32) * (2.0 * math.pi / length)
    window_taper = 0.5 - 0.5 * jnp.cos(sample_ids.astype(jnp.float32) * (2.0 * math.pi / length))
    factor = window_taper / math.sqrt(length)
    dft_table = jnp.concatenate([jnp.cos(angles) * factor, -jnp.sin(angles) * factor], axis=0)
    return dft_table.astype(jnp.bfloat16)


def unpack_flags(packed_words):
    shifts = jnp.arange(32, dtype=jnp.int32)
    bit_values = jnp.bitwise_and(
        jnp.right_shift(packed_words[:, :, None], shifts[None, None, :]), 1
    )
    return bit_values.reshape(packed_words.shape[0], packed_words.shape[1] * 32)


def whiten(records, band_bins, flags):
    bin_count = band_bins + 4
    dft_table = transform_table(records.shape[-1], bin_count)
    spectrum = jnp.einsum("cl,swl->scw", dft_table, records, preferred_element_type=jnp.float32)
    real_part = spectrum[:, :bin_count]
    imag_part = spectrum[:, bin_count:]
    magnitude = jnp.sqrt(real_part * real_part + imag_part * imag_part)
    smooth = (
        magnitude[:, 0:band_bins]
        + magnitude[:, 1 : band_bins + 1]
        + magnitude[:, 2 : band_bins + 2]
        + magnitude[:, 3 : band_bins + 3]
        + magnitude[:, 4 : band_bins + 4]
    ) / 5.0
    factor = flags[:, None, :] / jnp.maximum(smooth, FLOOR)
    whitened = jnp.concatenate(
        [real_part[:, 2 : band_bins + 2] * factor, imag_part[:, 2 : band_bins + 2] * factor], axis=2
    )
    return whitened.astype(jnp.bfloat16).transpose(1, 0, 2)


def exchange_kernel(
    spec_ref, word_ref, out_ref, words_ref,
    gathered, turned, block,
    plane_send, plane_recv, word_send, word_recv,
    up_send, up_recv, down_send, down_recv, far_send, far_recv, side_send, side_recv,
):
    tm = lax.axis_index("tm")
    freq = lax.axis_index("freq")
    y, zl = tm // 2, tm % 2
    mine = 2 * freq + zl

    def plane_peer(offset):
        other = (mine + offset) % PLANE
        return other, (2 * y + other % 2, other // 2)

    def ring_peer(offset):
        return (2 * ((y + offset) % Y) + zl, freq)

    barrier = pltpu.get_barrier_semaphore()
    for offset in range(1, PLANE):
        pl.semaphore_signal(barrier, inc=1, device_id=plane_peer(offset)[1], device_id_type=MESH)
    for offset in range(1, Y):
        pl.semaphore_signal(barrier, inc=1, device_id=ring_peer(offset), device_id_type=MESH)
    pl.semaphore_wait(barrier, PLANE - 1 + Y - 1)

    row_at = pl.multiple_of(freq * STA, STA)
    plane = []
    for offset in range(1, PLANE):
        other, device = plane_peer(offset)
        copy = pltpu.make_async_remote_copy(
            word_ref, words_ref.at[y, mine],
            word_send.at[offset], word_recv.at[offset], device_id=device, device_id_type=MESH)
        copy.start()
        plane.append(copy)
    for offset in range(1, PLANE):
        other, device = plane_peer(offset)
        copy = pltpu.make_async_remote_copy(
            spec_ref.at[other], gathered.at[y, zl, pl.ds(row_at, STA), :],
            plane_send.at[offset], plane_recv.at[offset], device_id=device, device_id_type=MESH)
        copy.start()
        plane.append(copy)
    gathered[y, zl, pl.ds(row_at, STA), :] = spec_ref[mine]
    words_ref[y, mine] = word_ref[...]
    for copy in plane:
        copy.wait()

    far = []
    for offset in range(1, Y):
        copy = pltpu.make_async_remote_copy(
            words_ref.at[y], words_ref.at[y],
            far_send.at[offset], far_recv.at[offset],
            device_id=ring_peer(offset), device_id_type=MESH)
        copy.start()
        far.append(copy)

    def piece(owner, shift):
        at = pl.multiple_of(((owner + shift) % Y) * ROWS, ROWS)
        return gathered.at[owner, :, pl.ds(at, ROWS), :]

    def ring_copy(plan, slot, step, send, recv):
        kind, shift = plan[slot]
        owner = y if kind == "own" else (y - step + Y) % Y
        ref = piece(owner, shift)
        return pltpu.make_async_remote_copy(
            ref, ref, send.at[slot], recv.at[slot],
            device_id=ring_peer(step % Y), device_id_type=MESH)

    ups = [ring_copy(UP, slot, 1, up_send, up_recv) for slot in range(6)]
    downs = [ring_copy(DOWN, slot, -1, down_send, down_recv) for slot in range(6)]

    def multiply(shift):
        at = pl.multiple_of(((y + shift) % Y) * ROWS, ROWS)
        right = jnp.concatenate(
            [gathered[owner, part, pl.ds(at, ROWS), :] for owner in range(Y) for part in range(2)], axis=1)
        both = lax.dot_general(turned[...], right, (((1,), (1,)), ((), ())),
                               preferred_element_type=jnp.float32)
        block[shift] = both.reshape(2, ROWS, ROWS)
        col = pl.multiple_of(((y + shift) % Y) * ROWS, ROWS)
        half = pl.multiple_of((1 - zl) * 128, 128)
        copy = pltpu.make_async_remote_copy(
            block.at[shift, :, pl.ds(half, 128), :],
            out_ref.at[zl, :, :, pl.ds(col, ROWS)],
            side_send.at[shift], side_recv.at[shift],
            device_id=(2 * y + 1 - zl, freq), device_id_type=MESH)
        copy.start()
        kept = pl.multiple_of(zl * 128, 128)
        out_ref[zl, :, :, pl.ds(col, ROWS)] = block[shift, :, pl.ds(kept, 128), :]
        return copy

    for slot in (0, 1):
        ups[slot].start()
        downs[slot].start()
    downs[0].wait_recv()
    downs[2].start()
    ups[0].wait_recv()
    ups[1].wait_recv()
    ups[2].start()
    downs[1].wait_recv()
    ups[3].start()
    downs[3].start()
    ups[4].start()
    downs[4].start()
    ups[5].start()
    downs[5].start()
    ups[2].wait_recv()
    downs[2].wait_recv()
    row = pl.multiple_of(y * ROWS, ROWS)
    for owner in range(Y):
        for part in range(2):
            left = gathered[owner, part, pl.ds(row, ROWS), :]
            lane = (2 * owner + part) * 256
            turned[0:ROWS, lane : lane + 256] = left
            turned[ROWS : 2 * ROWS, lane : lane + 256] = jnp.concatenate(
                [left[:, 128:], -left[:, :128]], axis=1)
    sides = [multiply(0), multiply(1)]
    ups[3].wait_recv()
    downs[3].wait_recv()
    ups[4].wait_recv()
    sides.append(multiply(3))
    downs[4].wait_recv()
    ups[5].wait_recv()
    downs[5].wait_recv()
    sides.append(multiply(2))
    for copy in far:
        copy.wait()
    for copy in ups + downs:
        copy.wait_send()
    for copy in sides:
        copy.wait()


def exchange(spectra, words):
    dma = pltpu.SemaphoreType.DMA
    vmem = pl.BlockSpec(memory_space=pltpu.VMEM)
    return pl.pallas_call(
        exchange_kernel,
        out_shape=(
            jax.ShapeDtypeStruct((2, 2, 128, 1024), jnp.float32),
            jax.ShapeDtypeStruct((Y, PLANE, 4, 128), jnp.int32),
        ),
        in_specs=[vmem, vmem],
        out_specs=(vmem, vmem),
        scratch_shapes=[
            pltpu.VMEM((Y, 2, 1024, 256), jnp.bfloat16),
            pltpu.VMEM((2 * ROWS, 2048), jnp.bfloat16),
            pltpu.VMEM((Y, 2, ROWS, ROWS), jnp.float32),
            dma((PLANE,)), dma((PLANE,)), dma((PLANE,)), dma((PLANE,)),
            dma((6,)), dma((6,)), dma((6,)), dma((6,)),
            dma((Y,)), dma((Y,)), dma((Y,)), dma((Y,)),
        ],
        compiler_params=pltpu.CompilerParams(
            collective_id=0, has_side_effects=True, vmem_limit_bytes=48 << 20),
    )(spectra, words)


def local(records, gap_flags, station_mask):
    kept_words = gap_flags * station_mask[:, None]
    here_flags = unpack_flags(kept_words).astype(jnp.float32)
    spectra = whiten(records, PLANE, here_flags)
    words = jnp.pad(kept_words.T, ((0, 0), (0, 128 - STA)))
    stacks, all_words = exchange(spectra, words)
    every = all_words[:, :, :, :STA].reshape(Y, 16, 2, 4, STA)
    every = every.transpose(1, 4, 0, 2, 3).reshape(1024, 32)
    every_flags = unpack_flags(every).astype(jnp.bfloat16)
    row_start = lax.axis_index("tm") * 128
    row_flags = lax.dynamic_slice_in_dim(every_flags, row_start, 128, 0)
    counts = jnp.dot(row_flags, every_flags.T, preferred_element_type=jnp.float32)
    return stacks / jnp.maximum(counts, 1.0)


def solution(mesh):
    placed = (P("freq", "tm", None), P("freq", "tm"), P("freq"))
    return jax.shard_map(
        local, mesh=mesh, in_specs=placed, out_specs=P("freq", None, "tm", None), check_vma=False
    )
```

time: 249 us -> 91.6 us (0.37)
  the two profiles are of different devices: /device:TPU:0 before, /device:TPU:64 now
where the time goes in v1:
time: 91.6 us; the launch traced here: 91.3 us
  Pallas kernels  74.1 us (81%)
  matrix products  8.18 us (9%)
  other arithmetic  6.39 us (7%)
  local copies, waits for them, and re-layouts  2.5 us (3%)
    pallas_call x1, Pallas kernels, exchange(): pl.pallas_call(exchange_kernel, out_shape=(jax.ShapeDtypeStruct((2, 2, 12...  74.1 us
    dot_general x1, matrix products, whiten(): jnp.einsum('cl,swl->scw', dft_table, records, preferred_element_type=jnp....  6.01 us
    dot_general x1, matrix products, local(): jnp.dot(row_flags, every_flags.T, preferred_element_type=jnp.float32)  2.17 us
    convert_element_type x1, other arithmetic, local(): every_flags = unpack_flags(every).astype(jnp.bfloat16)  1.87 us

profile of v1, /device:TPU:64, one launch (start us, length us, event | category | flops | bytes accessed | tf_op | source)
XLA Modules:
  0.0 91.3 jit_solution(12292316392699210230)
XLA Ops:
  0.0 0.3 multiply_convert_fusion.1
  0.4 6.0 %fusion.16 = f32[72,64,128]{2,0,1:T(8,128)S(1)} fusion(bf16[64,128,512]{2,1,0:T(8,128)(2,1)} %param.3, bf16[36,512]{1,0:T(8,128)(2,1)S(1)} %get-tuple-element.12, bf16[36,512]{1,0:T(8,128)(2,1)S(1)} %get-tuple-element.11), kind=kOutput, calls=%fused_computation.36 | convolution fusion | flops 604127232 | bytes 10821632 | tf_op jit(solution)/shard_map/cl,swl->scw/dot_general | solution.py:42
  6.4 0.5 copy.11
  6.9 0.0 copy-start
  6.9 0.0 copy-start.1
  6.9 0.4 fusion.3
  7.3 0.1 shift_right_arithmetic.49
  7.4 0.2 copy-done
  7.6 0.0 copy-done.1
  7.6 0.7 fusion.20
  8.3 1.5 %copy.7 = f32[64,128]{1,0:T(8,128)} copy(f32[64,128]{0,1:T(8,128)} %fusion.20) | data formatting | bytes 65536 | tf_op jit(solution)/shard_map/convert_element_type | solution.py:217
  9.8 1.1 %fusion.8 = (bf16[64,32,128]{2,0,1:T(8,128)(2,1)S(1)}, f32[64,32,128]{2,0,1:T(8,128)S(1)}) fusion(f32[64,72,128]{2,0,1:T(8,128)S(1)} %bitcast.35, f32[64,36,128]{2,0,1:T(8,128)S(1)} %fusion.3, f32[64,128]{1,0:T(8,128)} %copy.7), kind=kLoop, calls=%fused_computation.19 | loop fusion | flops 2359296 | bytes 7897088 | tf_op jit(solution)/shard_map/convert
  10.9 0.2 fusion.4
  11.1 0.1 maximum_bitcast_fusion.spec_ref
  11.3 74.1 %shard_map.37 = (f32[2,2,128,1024]{3,2,1,0:T(8,128)S(1)}, s32[4,32,4,128]{3,2,1,0:T(4,128)S(1)}) custom-call(bf16[32,64,256]{2,1,0:T(8,128)(2,1)S(1)} %maximum_bitcast_fusion.spec_ref, s32[4,128]{1,0:T(4,128)S(1)} %pad.4.word_ref), custom_call_target="tpu_custom_call" | custom-call | tf_op jit(solution)/shard_map/pallas_call | solution.py:194
  85.5 0.1 shift_right_arithmetic.52
  85.6 0.1 shift_right_arithmetic.56
  85.7 1.9 %fusion.1 = bf16[1024,1024]{0,1:T(8,128)(2,1)} fusion(s32[1024]{0:T(1024)S(1)} %shift_right_arithmetic.56, s32[1024,32]{0,1:T(8,128)S(1)} %shift_right_arithmetic.52), kind=kLoop, calls=%fused_computation.2 | loop fusion | flops 3145728 | bytes 2232320 | tf_op jit(solution)/shard_map/convert_element_type | solution.py:223
  87.6 2.2 %convolution_maximum_fusion = f32[128,1024]{1,0:T(8,128)S(1)} fusion(bf16[1024,1024]{0,1:T(8,128)(2,1)} %fusion.1, s32[]{:T(128)S(6)} %select_n.13), kind=kOutput, calls=%fused_computation.4 | convolution fusion | flops 268566528 | bytes 2883588 | tf_op jit(solution)/shard_map/dot_general | solution.py:226
  89.7 1.6 %broadcast_divide_fusion = f32[2,2,128,1024]{3,2,1,0:T(8,128)} fusion(f32[2,2,128,1024]{3,2,1,0:T(8,128)S(1)} %get-tuple-element.7, f32[128,1024]{1,0:T(8,128)S(1)} %convolution_maximum_fusion), kind=kLoop, calls=%fused_computation.21 | loop fusion | flops 524288 | bytes 4718592 | tf_op jit(solution)/shard_map/div | solution.py:227
  (7 shorter events, 0.1 us)
Async XLA Ops:
  6.9 0.7 copy-start
  6.9 0.7 copy-start.1

commit v2 on v0

v2 whole, which is shorter than its diff:
```python
import math

import jax
import jax.numpy as jnp
import numpy as np
from jax import lax
from jax.experimental import pallas as pl
from jax.experimental.pallas import tpu as pltpu
from jax.sharding import PartitionSpec as P

FLOOR = 0.25
MESH = pl.DeviceIdType.MESH
Y = 4
PLANE = 32
STA = 64
CHUNKS = 4
PART = STA // CHUNKS
WIN = 128
LEN = 512
ROWS = 256
SIDE = 128
SLOTS = 40
NT = (((1,), (1,)), ((), ()))
TN = (((0,), (0,)), ((), ()))
QUARTERS = tuple(("q", q) for q in range(CHUNKS))
WHOLE = ("w", 0)
FIRST, SECOND = ("h", 0), ("h", 1)
UP = (
    [("own", 1, q) for q in QUARTERS]
    + [("own", 2, q) for q in QUARTERS]
    + [("fwd", 2, q) for q in QUARTERS]
    + [("own", 0, WHOLE), ("fwd", 1, WHOLE), ("own", 3, FIRST), ("own", 3, SECOND)]
)
DOWN = (
    [("own", 3, q) for q in QUARTERS]
    + [("own", 0, q) for q in QUARTERS]
    + [("fwd", 3, q) for q in QUARTERS]
    + [("own", 2, WHOLE), ("own", 1, FIRST), ("fwd", 0, FIRST), ("own", 1, SECOND), ("fwd", 0, SECOND)]
)


def transform_table():
    t = np.arange(LEN)
    taper = (0.5 - 0.5 * np.cos(2.0 * math.pi * t / LEN)) / math.sqrt(LEN)
    table = np.zeros((2, 5, 8, LEN))
    for v in range(5):
        for i in range(8):
            b = 5 * i + v
            if b < 36:
                angle = 2.0 * math.pi * ((b * t) % LEN) / LEN
                table[0, v, i] = np.cos(angle) * taper
                table[1, v, i] = -np.sin(angle) * taper
    return jnp.asarray(table.reshape(2 * SLOTS, LEN).astype(np.float32)).astype(jnp.bfloat16)


def kernel(
    rec_hbm, table_ref, flag_ref, word_ref, out_ref, inv_ref,
    rec, usable, stage_re, stage_im, spec, gathered, turned, block, ring_words, all_words, flat_words, bits,
    rec_sem, plane_send, plane_recv, wring_send, wring_recv, wplane_send, wplane_recv,
    up_send, up_recv, down_send, down_recv, side_send, side_recv,
):
    tm = lax.axis_index("tm")
    freq = lax.axis_index("freq")
    y, zl = tm // 2, tm % 2
    mine = 2 * freq + zl

    def plane_device(other):
        return (2 * y + other % 2, other // 2)

    def ring_device(offset):
        return (2 * ((y + offset) % Y) + zl, freq)

    loads = []
    for q in range(CHUNKS):
        copy = pltpu.make_async_copy(
            rec_hbm.at[pl.ds(PART * q, PART)], rec.at[pl.ds(PART * q, PART)], rec_sem.at[q])
        copy.start()
        loads.append(copy)

    barrier = pltpu.get_barrier_semaphore()

    def greet(offset, carry):
        pl.semaphore_signal(
            barrier, inc=1, device_id=plane_device((mine + offset) % PLANE), device_id_type=MESH)
        return carry

    lax.fori_loop(1, PLANE, greet, 0)
    for offset in range(1, Y):
        pl.semaphore_signal(barrier, inc=1, device_id=ring_device(offset), device_id_type=MESH)

    lane = lax.broadcasted_iota(jnp.int32, (STA, WIN), 1)
    words = flag_ref[...]
    spread = jnp.broadcast_to(words[:, 0:1], (STA, WIN))
    for j in range(1, 4):
        spread = jnp.where(lane >= 32 * j, jnp.broadcast_to(words[:, j : j + 1], (STA, WIN)), spread)
    usable[...] = (lax.shift_right_logical(spread, lane % 32) & 1).astype(jnp.float32)

    def transform(q):
        def pair(n, carry):
            first = PART * q + 2 * n
            both = rec[pl.ds(first, 2)].reshape(2 * WIN, LEN)
            spectrum = lax.dot_general(table_ref[...], both, NT, preferred_element_type=jnp.float32)
            for s in range(2):
                re = [spectrum[8 * v : 8 * v + 8, WIN * s : WIN * (s + 1)] for v in range(5)]
                im = [spectrum[SLOTS + 8 * v : SLOTS + 8 * v + 8, WIN * s : WIN * (s + 1)] for v in range(5)]
                m = [jnp.sqrt(a * a + b * b) for a, b in zip(re, im)]

                def above(x):
                    return pltpu.roll(x, 7, 0)

                def below(x):
                    return pltpu.roll(x, 1, 0)

                low, high = m[0] + m[1], m[3] + m[4]
                sums = [
                    low + m[2] + below(high),
                    low + m[2] + m[3] + below(m[4]),
                    low + m[2] + high,
                    m[1] + m[2] + high + above(m[0]),
                    m[2] + high + above(low),
                ]
                keep = jnp.broadcast_to(usable[pl.ds(first + s, 1), :], (8, WIN))
                for v in range(5):
                    factor = keep / jnp.maximum(sums[v] * 0.2, FLOOR)
                    at = pl.multiple_of((2 * n + s) * SLOTS + 8 * v, 8)
                    stage_re[pl.ds(at, 8), :] = re[v] * factor
                    stage_im[pl.ds(at, 8), :] = im[v] * factor
            return carry

        lax.fori_loop(0, PART // 2, pair, 0)
        for p in range(PLANE):
            i, v = (p + 2) // 5, (p + 2) % 5
            for half, stage in ((0, stage_re), (1, stage_im)):
                rows = stage[pl.ds(8 * v + i, PART, stride=SLOTS), :]
                spec[p, PART * q : PART * (q + 1), WIN * half : WIN * (half + 1)] = rows.astype(jnp.bfloat16)

    def plane_copy(q, sender, receiver):
        at = pl.ds(PART * q, PART)
        return pltpu.make_async_remote_copy(
            spec.at[receiver, at, :], gathered.at[y, sender % 2, sender // 2, at, :],
            plane_send.at[q, receiver], plane_recv.at[q, sender],
            device_id=plane_device(receiver), device_id_type=MESH)

    def send_plane(q):
        def one(offset, carry):
            plane_copy(q, mine, (mine + offset) % PLANE).start()
            return carry

        lax.fori_loop(1, PLANE, one, 0)
        gathered[y, zl, freq, PART * q : PART * (q + 1), :] = spec[mine, PART * q : PART * (q + 1), :]

    def from_plane(q, shift):
        def one(i, carry):
            sender = 8 * ((y + shift) % Y) + i

            @pl.when(sender != mine)
            def _():
                plane_copy(q, sender, (sender + 1) % PLANE).wait_recv()

            return carry

        lax.fori_loop(0, 8, one, 0)

    for q in range(CHUNKS):
        loads[q].wait()
        transform(q)
        if q == 0:
            pl.semaphore_wait(barrier, PLANE - 1 + Y - 1)
        send_plane(q)

    ring_words[y] = word_ref[...]
    word_ring = [
        pltpu.make_async_remote_copy(
            word_ref, ring_words.at[y], wring_send.at[offset], wring_recv.at[offset],
            device_id=ring_device(offset), device_id_type=MESH)
        for offset in range(1, Y)
    ]
    for copy in word_ring:
        copy.start()

    def message(entry, slot, step, send, recv):
        kind, shift, (how, n) = entry
        owner = y if kind == "own" else (y - step + Y) % Y
        group = 4 * ((owner + shift) % Y)
        if how == "q":
            ref = gathered.at[owner, :, pl.ds(group, 4), pl.ds(PART * n, PART), :]
        elif how == "h":
            ref = gathered.at[owner, :, pl.ds(group + 2 * n, 2), :, :]
        else:
            ref = gathered.at[owner, :, pl.ds(group, 4), :, :]
        return pltpu.make_async_remote_copy(
            ref, ref, send.at[slot], recv.at[slot],
            device_id=ring_device(step % Y), device_id_type=MESH)

    ups = [message(entry, slot, 1, up_send, up_recv) for slot, entry in enumerate(UP)]
    downs = [message(entry, slot, -1, down_send, down_recv) for slot, entry in enumerate(DOWN)]

    for q in range(CHUNKS):
        from_plane(q, 1)
        ups[q].start()
        from_plane(q, 3)
        downs[q].start()
        from_plane(q, 2)
        ups[4 + q].start()
        from_plane(q, 0)
        downs[4 + q].start()
        if q == 0:
            for copy in word_ring:
                copy.wait()

            def word_copy(sender, receiver):
                return pltpu.make_async_remote_copy(
                    ring_words, all_words.at[sender],
                    wplane_send.at[receiver], wplane_recv.at[sender],
                    device_id=plane_device(receiver), device_id_type=MESH)

            def send_words(offset, carry):
                word_copy(mine, (mine + offset) % PLANE).start()
                return carry

            lax.fori_loop(1, PLANE, send_words, 0)
            all_words[mine] = ring_words[...]

    for q in range(CHUNKS):
        ups[4 + q].wait_recv()
        ups[8 + q].start()
        downs[q].wait_recv()
        downs[8 + q].start()
    ups[12].start()
    downs[12].start()
    for q in range(CHUNKS):
        ups[q].wait_recv()
    ups[13].start()
    downs[13].start()
    for q in range(CHUNKS):
        downs[4 + q].wait_recv()
    downs[14].start()
    ups[14].start()
    downs[15].start()
    downs[16].start()
    ups[15].start()

    def words_here(offset, carry):
        sender = (mine + offset) % PLANE
        word_copy(sender, sender).wait_recv()
        return carry

    lax.fori_loop(1, PLANE, words_here, 0)
    lane2 = lax.broadcasted_iota(jnp.int32, (2, WIN), 1)
    for owner in range(Y):
        for part in range(2):
            base = 4 * (2 * owner + part)
            for g in range(8):
                a = all_words[4 * g + part, owner]
                b = all_words[4 * g + 2 + part, owner]
                flat_words[base : base + 2, WIN * g : WIN * (g + 1)] = jnp.where(
                    lane2 < 64, a, pltpu.roll(b, 64, 1))
                flat_words[base + 2 : base + 4, WIN * g : WIN * (g + 1)] = jnp.where(
                    lane2 < 64, pltpu.roll(a, 64, 1), b)
    shifts = lax.broadcasted_iota(jnp.int32, (32, 1024), 0)

    def unpack(n, carry):
        row = jnp.broadcast_to(flat_words[pl.ds(n, 1), :], (32, 1024))
        bit = (lax.shift_right_logical(row, shifts) & 1).astype(jnp.float32)
        bits[pl.ds(pl.multiple_of(32 * n, 32), 32), :] = bit.astype(jnp.bfloat16)
        return carry

    lax.fori_loop(0, 32, unpack, 0)
    here = bits[:, pl.ds(pl.multiple_of(tm * SIDE, SIDE), SIDE)]
    counts = lax.dot_general(here, bits[...], TN, preferred_element_type=jnp.float32)
    inv_ref[...] = 1.0 / jnp.maximum(counts, 1.0)

    def multiply(shift, half=None):
        base = (y + shift) % Y
        count = 4 if half is None else 2
        width = STA * count
        group = 4 * base + (0 if half is None else 2 * half)
        right = jnp.concatenate(
            [gathered[owner, part, pl.ds(group, count)].reshape(width, 2 * WIN)
             for owner in range(Y) for part in range(2)], axis=1)
        both = lax.dot_general(turned[...], right, NT, preferred_element_type=jnp.float32)
        at = 0 if not half else width
        slot = shift if half is None else shift + 2 * half
        block[shift, :, :, at : at + width] = both.reshape(2, ROWS, width)
        col = pl.multiple_of(group * STA, SIDE)
        away = pl.multiple_of((1 - zl) * SIDE, SIDE)
        copy = pltpu.make_async_remote_copy(
            block.at[shift, :, pl.ds(away, SIDE), at : at + width],
            out_ref.at[zl, :, :, pl.ds(col, width)],
            side_send.at[slot], side_recv.at[slot],
            device_id=(2 * y + 1 - zl, freq), device_id_type=MESH)
        copy.start()
        kept = pl.multiple_of(zl * SIDE, SIDE)
        out_ref[zl, :, :, pl.ds(col, width)] = block[shift, :, pl.ds(kept, SIDE), at : at + width]
        return copy

    for q in range(CHUNKS):
        ups[8 + q].wait_recv()
        downs[8 + q].wait_recv()
    for owner in range(Y):
        for part in range(2):
            left = gathered[owner, part, pl.ds(4 * y, 4)].reshape(ROWS, 2 * WIN)
            at = (2 * owner + part) * 256
            turned[0:ROWS, at : at + 256] = left
            turned[ROWS : 2 * ROWS, at : at + 256] = jnp.concatenate(
                [left[:, WIN:], -left[:, :WIN]], axis=1)
    sides = [multiply(0), multiply(1)]
    ups[12].wait_recv()
    downs[12].wait_recv()
    ups[13].wait_recv()
    sides.append(multiply(3))
    downs[13].wait_recv()
    downs[14].wait_recv()
    ups[14].wait_recv()
    sides.append(multiply(2, 0))
    downs[15].wait_recv()
    downs[16].wait_recv()
    ups[15].wait_recv()
    sides.append(multiply(2, 1))

    def sent(offset, carry):
        other = (mine + offset) % PLANE
        for q in range(CHUNKS):
            plane_copy(q, mine, other).wait_send()
        word_copy(mine, other).wait_send()
        return carry

    lax.fori_loop(1, PLANE, sent, 0)
    for copy in ups + downs:
        copy.wait_send()
    for copy in sides:
        copy.wait()


def stack_up(records, table, flags, words):
    dma = pltpu.SemaphoreType.DMA
    vmem = pl.BlockSpec(memory_space=pltpu.VMEM)
    return pl.pallas_call(
        kernel,
        out_shape=(
            jax.ShapeDtypeStruct((2, 2, SIDE, 1024), jnp.float32),
            jax.ShapeDtypeStruct((SIDE, 1024), jnp.float32),
        ),
        in_specs=[pl.BlockSpec(memory_space=pl.ANY), vmem, vmem, vmem],
        out_specs=(vmem, vmem),
        scratch_shapes=[
            pltpu.VMEM((STA, WIN, LEN), jnp.bfloat16),
            pltpu.VMEM((STA, WIN), jnp.float32),
            pltpu.VMEM((PART * SLOTS, WIN), jnp.float32),
            pltpu.VMEM((PART * SLOTS, WIN), jnp.float32),
            pltpu.VMEM((PLANE, STA, 2 * WIN), jnp.bfloat16),
            pltpu.VMEM((Y, 2, 16, STA, 2 * WIN), jnp.bfloat16),
            pltpu.VMEM((2 * ROWS, 2048), jnp.bfloat16),
            pltpu.VMEM((Y, 2, ROWS, ROWS), jnp.float32),
            pltpu.VMEM((Y, 2, WIN), jnp.int32),
            pltpu.VMEM((PLANE, Y, 2, WIN), jnp.int32),
            pltpu.VMEM((PLANE, 1024), jnp.int32),
            pltpu.VMEM((1024, 1024), jnp.bfloat16),
            dma((CHUNKS,)), dma((CHUNKS, PLANE)), dma((CHUNKS, PLANE)),
            dma((Y,)), dma((Y,)), dma((PLANE,)), dma((PLANE,)),
            dma((len(UP),)), dma((len(UP),)), dma((len(DOWN),)), dma((len(DOWN),)),
            dma((5,)), dma((5,)),
        ],
        compiler_params=pltpu.CompilerParams(
            collective_id=0, has_side_effects=True, vmem_limit_bytes=56 << 20),
    )(records, table, flags, words)


def local(records, gap_flags, station_mask):
    kept = gap_flags * station_mask[:, None]
    words = kept.T.reshape(2, WIN)
    stacks, inverse = stack_up(records, transform_table(), kept, words)
    return stacks * inverse


def solution(mesh):
    placed = (P("freq", "tm", None), P("freq", "tm"), P("freq"))
    return jax.shard_map(
        local, mesh=mesh, in_specs=placed, out_specs=P("freq", None, "tm", None), check_vma=False
    )
```

time: 249 us -> 73.9 us (0.30)
  waiting for transfers between devices: 178 us -> 0 us
  Pallas kernels: 0 us -> 66.7 us
  starting transfers between devices: 20 us -> 0 us
  matrix products: 14.7 us -> 0 us
  local copies, waits for them, and re-layouts: 15.5 us -> 1.52 us
  between operations: 13.6 us -> 0.01 us
    all_gather x1 -> x0, waiting for transfers between devices: 155 us -> none  [local(): window_part = lax.all_gather(masked, 'tm', axis=3, tiled=True)]
    pallas_call x0 -> x1, Pallas kernels: none -> 66.7 us  [stack_up(): pl.pallas_call(kernel, out_shape=(jax.ShapeDtypeStruct((2, 2, SIDE, 1024)...]
    all_to_all x3 -> x0, waiting for transfers between devices: 23 us -> none  [the longest x1 16.2 us: local(): lax.all_to_all(whitened, 'freq', split_axis=1, concat_axis=0, tiled=True)]
    all_to_all x3 -> x0, starting transfers between devices: 20 us -> none  [the longest x2 12.8 us: sent_to_all(): return lax.all_to_all(copies, axis, split_axis=0, concat_axis=0, tiled=True)]
    dot_general x4 -> x0, matrix products: 14.7 us -> none  [the longest x1 6.01 us: whiten(): jnp.einsum('cl,swl->scw', dft_table, records, preferred_element_type=jnp....]
    reshape x2 -> x1, local copies, waits for them, and re-layouts: 8.15 us -> 0.67 us  [local(): words = kept.T.reshape(2, WIN)]
    mul x2, other arithmetic: 1.82 us -> 4.7 us  [the longest x1 3.36 us: local(): return stacks * inverse]
  transfers between devices with their start and end apart: 4 -> 0, of which waited for: 3 -> 0; matrix products, arithmetic and copies ran while one was open for 5% -> 0% of each run, Pallas kernels for 0% -> 0%
where the time goes in v2:
time: 73.9 us; the launch traced here: 73.7 us
  Pallas kernels  66.7 us (90%)
  other arithmetic  5.43 us (7%)
  local copies, waits for them, and re-layouts  1.52 us (2%)
    pallas_call x1, Pallas kernels, stack_up(): pl.pallas_call(kernel, out_shape=(jax.ShapeDtypeStruct((2, 2, SIDE, 1024)...  66.7 us
    mul x1, other arithmetic, local(): return stacks * inverse  3.36 us

profile of v2, /device:TPU:0, one launch (start us, length us, event | category | flops | bytes accessed | tf_op | source)
XLA Modules:
  0.0 73.7 jit_solution(11987758606535590915)
XLA Ops:
  0.0 0.8 %copy.5 = s32[64,4]{1,0:T(8,128)S(1)} copy(s32[64,4]{0,1:T(4,128)} %param.5) | data formatting | bytes 2048 | tf_op args[1]
  0.8 0.7 fusion
  1.5 0.1 copy.6
  1.6 0.7 reshape.5.word_ref
  2.2 1.3 %broadcast_multiply_fusion.1.flag_ref = s32[64,4]{1,0:T(8,128)} fusion(s32[64,4]{1,0:T(8,128)S(1)} %copy.5, s32[64]{0:T(128)} %param.6), kind=kLoop, calls=%fused_computation.1 | loop fusion | flops 256 | bytes 2304 | tf_op jit(solution)/shard_map/mul | solution.py:370
  3.6 66.7 %shard_map.46 = (f32[2,2,128,1024]{3,2,1,0:T(8,128)}, f32[128,1024]{1,0:T(8,128)}) custom-call(bf16[64,128,512]{2,1,0:T(8,128)(2,1)} %rec_hbm.1, bf16[80,512]{1,0:T(8,128)(2,1)} %constant.4.table_ref, s32[64,4]{1,0:T(8,128)} %broadcast_multiply_fusion.1.flag_ref, s32[2,128]{1,0:T(2,128)} %reshape.5.word_ref), custom_call_target="tpu_custom_call" | custom-call | tf_op jit(solution)/shard_map/pallas_call | solution.py:338
  70.3 3.4 %broadcast_multiply_fusion = f32[2,2,128,1024]{3,2,1,0:T(8,128)} fusion(f32[2,2,128,1024]{3,2,1,0:T(8,128)} %get-tuple-element.7, f32[128,1024]{1,0:T(8,128)} %get-tuple-element.8), kind=kLoop, calls=%fused_computation | loop fusion | flops 524288 | bytes 4718592 | tf_op jit(solution)/shard_map/mul | solution.py:373

commit v3 on v2

--- a/solution.py
+++ b/solution.py
@@ -19,23 +19,23 @@
 LEN = 512
 ROWS = 256
 SIDE = 128
+STEP = 4
 SLOTS = 40
 NT = (((1,), (1,)), ((), ()))
 TN = (((0,), (0,)), ((), ()))
 QUARTERS = tuple(("q", q) for q in range(CHUNKS))
-WHOLE = ("w", 0)
 FIRST, SECOND = ("h", 0), ("h", 1)
 UP = (
     [("own", 1, q) for q in QUARTERS]
     + [("own", 2, q) for q in QUARTERS]
     + [("fwd", 2, q) for q in QUARTERS]
-    + [("own", 0, WHOLE), ("fwd", 1, WHOLE), ("own", 3, FIRST), ("own", 3, SECOND)]
+    + [("own", 3, FIRST), ("own", 3, SECOND)]
 )
 DOWN = (
     [("own", 3, q) for q in QUARTERS]
     + [("own", 0, q) for q in QUARTERS]
     + [("fwd", 3, q) for q in QUARTERS]
-    + [("own", 2, WHOLE), ("own", 1, FIRST), ("fwd", 0, FIRST), ("own", 1, SECOND), ("fwd", 0, SECOND)]
+    + [("own", 1, FIRST), ("fwd", 0, FIRST), ("own", 1, SECOND), ("fwd", 0, SECOND)]
 )
 
 
@@ -54,10 +54,12 @@
 
 
 def kernel(
-    rec_hbm, table_ref, flag_ref, word_ref, out_ref, inv_ref,
-    rec, usable, stage_re, stage_im, spec, gathered, turned, block, ring_words, all_words, flat_words, bits,
+    rec_hbm, table_ref, flag_ref, mask_ref, out_ref,
+    rec, kept, square, word_ref, usable, stage_re, stage_im, spec, gathered, turned, block,
+    ring_words, all_words, flat_words, bits, inverse, side_out, side_in, mirror_out, mirror_in,
+    side_scale_out, side_scale_in, mirror_scale_out, mirror_scale_in,
     rec_sem, plane_send, plane_recv, wring_send, wring_recv, wplane_send, wplane_recv,
-    up_send, up_recv, down_send, down_recv, side_send, side_recv,
+    up_send, up_recv, down_send, down_recv, side_send, side_recv, mirror_send, mirror_recv,
 ):
     tm = lax.axis_index("tm")
     freq = lax.axis_index("freq")
@@ -70,6 +72,9 @@
     def ring_device(offset):
         return (2 * ((y + offset) % Y) + zl, freq)
 
+    def cross_device(offset):
+        return (2 * ((y + offset) % Y) + 1 - zl, freq)
+
     loads = []
     for q in range(CHUNKS):
         copy = pltpu.make_async_copy(
@@ -87,20 +92,31 @@
     lax.fori_loop(1, PLANE, greet, 0)
     for offset in range(1, Y):
         pl.semaphore_signal(barrier, inc=1, device_id=ring_device(offset), device_id_type=MESH)
-
+    for offset in (1, Y - 1):
+        pl.semaphore_signal(barrier, inc=1, device_id=cross_device(offset), device_id_type=MESH)
+
+    kept[...] = jnp.zeros_like(kept)
+    kept[0:4, 0:STA] = flag_ref[...] * mask_ref[...]
+    square[...] = jnp.zeros_like(square)
+    square[0:8, :] = kept[...]
+    words = jnp.transpose(square[...])[0:STA]
     lane = lax.broadcasted_iota(jnp.int32, (STA, WIN), 1)
-    words = flag_ref[...]
     spread = jnp.broadcast_to(words[:, 0:1], (STA, WIN))
     for j in range(1, 4):
         spread = jnp.where(lane >= 32 * j, jnp.broadcast_to(words[:, j : j + 1], (STA, WIN)), spread)
     usable[...] = (lax.shift_right_logical(spread, lane % 32) & 1).astype(jnp.float32)
+    low = lax.broadcasted_iota(jnp.int32, (1, WIN), 1) < STA
+    rows = kept[...]
+    rolled = pltpu.roll(rows, STA, 1)
+    word_ref[0:1] = jnp.where(low, rows[0:1], rolled[1:2])
+    word_ref[1:2] = jnp.where(low, rows[2:3], rolled[3:4])
 
     def transform(q):
         def pair(n, carry):
-            first = PART * q + 2 * n
-            both = rec[pl.ds(first, 2)].reshape(2 * WIN, LEN)
+            first = PART * q + STEP * n
+            both = rec[pl.ds(first, STEP)].reshape(STEP * WIN, LEN)
             spectrum = lax.dot_general(table_ref[...], both, NT, preferred_element_type=jnp.float32)
-            for s in range(2):
+            for s in range(STEP):
                 re = [spectrum[8 * v : 8 * v + 8, WIN * s : WIN * (s + 1)] for v in range(5)]
                 im = [spectrum[SLOTS + 8 * v : SLOTS + 8 * v + 8, WIN * s : WIN * (s + 1)] for v in range(5)]
                 m = [jnp.sqrt(a * a + b * b) for a, b in zip(re, im)]
@@ -122,12 +138,12 @@
                 keep = jnp.broadcast_to(usable[pl.ds(first + s, 1), :], (8, WIN))
                 for v in range(5):
                     factor = keep / jnp.maximum(sums[v] * 0.2, FLOOR)
-                    at = pl.multiple_of((2 * n + s) * SLOTS + 8 * v, 8)
+                    at = pl.multiple_of((STEP * n + s) * SLOTS + 8 * v, 8)
                     stage_re[pl.ds(at, 8), :] = re[v] * factor
                     stage_im[pl.ds(at, 8), :] = im[v] * factor
             return carry
 
-        lax.fori_loop(0, PART // 2, pair, 0)
+        lax.fori_loop(0, PART // STEP, pair, 0)
         for p in range(PLANE):
             i, v = (p + 2) // 5, (p + 2) % 5
             for half, stage in ((0, stage_re), (1, stage_im)):
@@ -165,7 +181,7 @@
         loads[q].wait()
         transform(q)
         if q == 0:
-            pl.semaphore_wait(barrier, PLANE - 1 + Y - 1)
+            pl.semaphore_wait(barrier, PLANE - 1 + Y - 1 + 2)
         send_plane(q)
 
     ring_words[y] = word_ref[...]
@@ -184,10 +200,8 @@
         group = 4 * ((owner + shift) % Y)
         if how == "q":
             ref = gathered.at[owner, :, pl.ds(group, 4), pl.ds(PART * n, PART), :]
-        elif how == "h":
+        else:
             ref = gathered.at[owner, :, pl.ds(group + 2 * n, 2), :, :]
-        else:
-            ref = gathered.at[owner, :, pl.ds(group, 4), :, :]
         return pltpu.make_async_remote_copy(
             ref, ref, send.at[slot], recv.at[slot],
             device_id=ring_device(step % Y), device_id_type=MESH)
@@ -229,16 +243,10 @@
     ups[12].start()
     downs[12].start()
     for q in range(CHUNKS):
-        ups[q].wait_recv()
-    ups[13].start()
+        downs[4 + q].wait_recv()
     downs[13].start()
-    for q in range(CHUNKS):
-        downs[4 + q].wait_recv()
     downs[14].start()
-    ups[14].start()
     downs[15].start()
-    downs[16].start()
-    ups[15].start()
 
     def words_here(offset, carry):
         sender = (mine + offset) % PLANE
@@ -266,35 +274,51 @@
         return carry
 
     lax.fori_loop(0, 32, unpack, 0)
-    here = bits[:, pl.ds(pl.multiple_of(tm * SIDE, SIDE), SIDE)]
+    here = bits[:, pl.ds(pl.multiple_of(y * ROWS, ROWS), ROWS)]
     counts = lax.dot_general(here, bits[...], TN, preferred_element_type=jnp.float32)
-    inv_ref[...] = 1.0 / jnp.maximum(counts, 1.0)
+    inverse[...] = 1.0 / jnp.maximum(counts, 1.0)
+    kept_at = pl.multiple_of(zl * SIDE, SIDE)
+    away_at = pl.multiple_of((1 - zl) * SIDE, SIDE)
+
+    def encode(values):
+        top = jnp.maximum(jnp.max(jnp.abs(values), axis=0, keepdims=True), 1e-30)
+        codes = jnp.round(values * (32767.0 / top)).astype(jnp.int32).astype(jnp.int16)
+        return codes, top / 32767.0
+
+    def decode(codes, scale):
+        return codes.astype(jnp.int32).astype(jnp.float32) * scale
 
     def multiply(shift, half=None):
-        base = (y + shift) % Y
         count = 4 if half is None else 2
         width = STA * count
-        group = 4 * base + (0 if half is None else 2 * half)
+        group = 4 * ((y + shift) % Y) + (0 if half is None else 2 * half)
         right = jnp.concatenate(
             [gathered[owner, part, pl.ds(group, count)].reshape(width, 2 * WIN)
              for owner in range(Y) for part in range(2)], axis=1)
         both = lax.dot_general(turned[...], right, NT, preferred_element_type=jnp.float32)
-        at = 0 if not half else width
-        slot = shift if half is None else shift + 2 * half
-        block[shift, :, :, at : at + width] = both.reshape(2, ROWS, width)
+        at = slice(SIDE, ROWS) if half == 1 else slice(0, width)
+        slot = shift if half is None else shift + half
         col = pl.multiple_of(group * STA, SIDE)
-        away = pl.multiple_of((1 - zl) * SIDE, SIDE)
-        copy = pltpu.make_async_remote_copy(
-            block.at[shift, :, pl.ds(away, SIDE), at : at + width],
-            out_ref.at[zl, :, :, pl.ds(col, width)],
-            side_send.at[slot], side_recv.at[slot],
-            device_id=(2 * y + 1 - zl, freq), device_id_type=MESH)
-        copy.start()
-        kept = pl.multiple_of(zl * SIDE, SIDE)
-        out_ref[zl, :, :, pl.ds(col, width)] = block[shift, :, pl.ds(kept, SIDE), at : at + width]
-        return copy
-
-    for q in range(CHUNKS):
+        scale = inverse[:, pl.ds(col, width)]
+        block[shift, :, :, at] = both.reshape(2, ROWS, width) * scale
+        for plane in range(2):
+            side_out[shift, plane, :, at], side_scale_out[slot, plane : plane + 1, 0:width] = encode(
+                block[shift, plane, pl.ds(away_at, SIDE), at])
+        copies = [
+            pltpu.make_async_remote_copy(
+                source, target, side_send.at[kind, slot], side_recv.at[kind, slot],
+                device_id=(2 * y + 1 - zl, freq), device_id_type=MESH)
+            for kind, (source, target) in enumerate((
+                (side_scale_out.at[slot], side_scale_in.at[slot]),
+                (side_out.at[shift, :, :, at], side_in.at[shift, :, :, at])))
+        ]
+        for copy in copies:
+            copy.start()
+        out_ref[zl, :, :, pl.ds(col, width)] = block[shift, :, pl.ds(kept_at, SIDE), at]
+        return copies
+
+    for q in range(CHUNKS):
+        ups[q].wait_recv()
         ups[8 + q].wait_recv()
         downs[8 + q].wait_recv()
     for owner in range(Y):
@@ -304,18 +328,31 @@
             turned[0:ROWS, at : at + 256] = left
             turned[ROWS : 2 * ROWS, at : at + 256] = jnp.concatenate(
                 [left[:, WIN:], -left[:, :WIN]], axis=1)
-    sides = [multiply(0), multiply(1)]
+    sides = [multiply(1)]
+    for plane, sign in ((0, 1.0), (1, -1.0)):
+        flipped = sign * jnp.transpose(block[1, plane])
+        for h in range(2):
+            mirror_out[h, plane], mirror_scale_out[h, plane : plane + 1] = encode(
+                flipped[SIDE * h : SIDE * (h + 1)])
+    mirrors = [
+        pltpu.make_async_remote_copy(
+            source.at[part], target.at[zl],
+            mirror_send.at[kind, n], mirror_recv.at[kind, n], device_id=device, device_id_type=MESH)
+        for n, (part, device) in enumerate(((zl, ring_device(1)), (1 - zl, cross_device(1))))
+        for kind, (source, target) in enumerate(
+            ((mirror_scale_out, mirror_scale_in), (mirror_out, mirror_in)))
+    ]
+    for copy in mirrors:
+        copy.start()
+    ups[13].start()
+    sides.append(multiply(0))
     ups[12].wait_recv()
     downs[12].wait_recv()
+    downs[13].wait_recv()
+    sides.append(multiply(2, 0))
     ups[13].wait_recv()
-    sides.append(multiply(3))
-    downs[13].wait_recv()
     downs[14].wait_recv()
-    ups[14].wait_recv()
-    sides.append(multiply(2, 0))
     downs[15].wait_recv()
-    downs[16].wait_recv()
-    ups[15].wait_recv()
     sides.append(multiply(2, 1))
 
     def sent(offset, carry):
@@ -328,49 +365,77 @@
     lax.fori_loop(1, PLANE, sent, 0)
     for copy in ups + downs:
         copy.wait_send()
-    for copy in sides:
+
+    def column(shift):
+        return pl.ds(pl.multiple_of(((y + shift) % Y) * ROWS, ROWS), ROWS)
+
+    for shift in (1, 0):
+        for copy in sides[1 - shift]:
+            copy.wait()
+        for plane in range(2):
+            out_ref[1 - zl, plane, :, column(shift)] = decode(
+                side_in[shift, plane], side_scale_in[shift, plane : plane + 1])
+    for copy in mirrors:
         copy.wait()
-
-
-def stack_up(records, table, flags, words):
+    for n in range(2):
+        for plane in range(2):
+            out_ref[n, plane, :, column(3)] = decode(
+                mirror_in[n, plane], mirror_scale_in[n, plane : plane + 1])
+    for half in range(2):
+        for copy in sides[2 + half]:
+            copy.wait()
+        at = slice(SIDE * half, SIDE * (half + 1))
+        col = pl.multiple_of(((y + 2) % Y) * ROWS + SIDE * half, SIDE)
+        for plane in range(2):
+            out_ref[1 - zl, plane, :, pl.ds(col, SIDE)] = decode(
+                side_in[2, plane, :, at], side_scale_in[2 + half, plane : plane + 1, 0:SIDE])
+
+
+def stack_up(records, table, flags, mask):
     dma = pltpu.SemaphoreType.DMA
     vmem = pl.BlockSpec(memory_space=pltpu.VMEM)
     return pl.pallas_call(
         kernel,
-        out_shape=(
-            jax.ShapeDtypeStruct((2, 2, SIDE, 1024), jnp.float32),
-            jax.ShapeDtypeStruct((SIDE, 1024), jnp.float32),
-        ),
-        in_specs=[pl.BlockSpec(memory_space=pl.ANY), vmem, vmem, vmem],
-        out_specs=(vmem, vmem),
+        out_shape=jax.ShapeDtypeStruct((2, 2, SIDE, 1024), jnp.float32),
+        in_specs=[pl.BlockSpec(memory_space=pltpu.HBM), vmem, vmem, vmem],
+        out_specs=vmem,
         scratch_shapes=[
             pltpu.VMEM((STA, WIN, LEN), jnp.bfloat16),
+            pltpu.VMEM((8, WIN), jnp.int32),
+            pltpu.VMEM((WIN, WIN), jnp.int32),
+            pltpu.VMEM((2, WIN), jnp.int32),
             pltpu.VMEM((STA, WIN), jnp.float32),
             pltpu.VMEM((PART * SLOTS, WIN), jnp.float32),
             pltpu.VMEM((PART * SLOTS, WIN), jnp.float32),
             pltpu.VMEM((PLANE, STA, 2 * WIN), jnp.bfloat16),
             pltpu.VMEM((Y, 2, 16, STA, 2 * WIN), jnp.bfloat16),
             pltpu.VMEM((2 * ROWS, 2048), jnp.bfloat16),
-            pltpu.VMEM((Y, 2, ROWS, ROWS), jnp.float32),
+            pltpu.VMEM((3, 2, ROWS, ROWS), jnp.float32),
             pltpu.VMEM((Y, 2, WIN), jnp.int32),
             pltpu.VMEM((PLANE, Y, 2, WIN), jnp.int32),
             pltpu.VMEM((PLANE, 1024), jnp.int32),
             pltpu.VMEM((1024, 1024), jnp.bfloat16),
+            pltpu.VMEM((ROWS, 1024), jnp.float32),
+            pltpu.VMEM((3, 2, SIDE, ROWS), jnp.int16),
+            pltpu.VMEM((3, 2, SIDE, ROWS), jnp.int16),
+            pltpu.VMEM((2, 2, SIDE, ROWS), jnp.int16),
+            pltpu.VMEM((2, 2, SIDE, ROWS), jnp.int16),
+            pltpu.VMEM((4, 2, ROWS), jnp.float32),
+            pltpu.VMEM((4, 2, ROWS), jnp.float32),
+            pltpu.VMEM((2, 2, ROWS), jnp.float32),
+            pltpu.VMEM((2, 2, ROWS), jnp.float32),
             dma((CHUNKS,)), dma((CHUNKS, PLANE)), dma((CHUNKS, PLANE)),
             dma((Y,)), dma((Y,)), dma((PLANE,)), dma((PLANE,)),
             dma((len(UP),)), dma((len(UP),)), dma((len(DOWN),)), dma((len(DOWN),)),
-            dma((5,)), dma((5,)),
+            dma((2, 4)), dma((2, 4)), dma((2, 2)), dma((2, 2)),
         ],
         compiler_params=pltpu.CompilerParams(
-            collective_id=0, has_side_effects=True, vmem_limit_bytes=56 << 20),
-    )(records, table, flags, words)
+            collective_id=0, has_side_effects=True, vmem_limit_bytes=48 << 20),
+    )(records, table, flags, mask)
 
 
 def local(records, gap_flags, station_mask):
-    kept = gap_flags * station_mask[:, None]
-    words = kept.T.reshape(2, WIN)
-    stacks, inverse = stack_up(records, transform_table(), kept, words)
-    return stacks * inverse
+    return stack_up(records, transform_table(), gap_flags.T, station_mask[None])
 
 
 def solution(mesh):

time: 73.9 us -> 58 us (0.78)
  Pallas kernels: 66.7 us -> 54.3 us
  other arithmetic: 5.43 us -> 0 us
  local copies, waits for them, and re-layouts: 1.52 us -> 3.54 us
    pallas_call x1, Pallas kernels: 66.7 us -> 54.3 us  [stack_up(): pl.pallas_call(kernel, out_shape=jax.ShapeDtypeStruct((2, 2, SIDE, 1024),...]
    mul x2 -> x0, other arithmetic: 4.7 us -> none  [the longest x1 3.36 us: local(): return stacks * inverse]
    unnamed x1 -> x7, local copies, waits for them, and re-layouts: 0.77 us -> 3.54 us
where the time goes in v3:
time: 58 us; the launch traced here: 57.9 us
  Pallas kernels  54.3 us (94%)
  local copies, waits for them, and re-layouts  3.54 us (6%)
    pallas_call x1, Pallas kernels, stack_up(): pl.pallas_call(kernel, out_shape=jax.ShapeDtypeStruct((2, 2, SIDE, 1024),...  54.3 us
    unnamed x7, local copies, waits for them, and re-layouts  3.54 us

profile of v3, /device:TPU:0, one launch (start us, length us, event | category | flops | bytes accessed | tf_op | source)
XLA Modules:
  0.0 57.9 jit_solution(5460444410038634744)
XLA Ops:
  0.0 0.0 copy-start
  0.0 0.9 %copy-done = bf16[80,512]{1,0:T(8,128)(2,1)S(1)} copy-done((bf16[80,512]{1,0:T(8,128)(2,1)S(1)}, bf16[80,512]{1,0:T(8,128)(2,1)}, u32[]{:S(2)}) %copy-start) | copy-done | bytes 81944
  0.9 0.0 copy-start.1
  0.9 0.7 %copy-done.1 = s32[64,4]{0,1:T(4,128)S(1)} copy-done((s32[64,4]{0,1:T(4,128)S(1)}, s32[64,4]{0,1:T(4,128)}, u32[]{:S(2)}) %copy-start.1) | copy-done | bytes 1048
  1.6 0.0 copy-start.2
  1.6 0.7 %copy-done.2 = s32[64]{0:T(128)S(1)} copy-done((s32[64]{0:T(128)S(1)}, s32[64]{0:T(128)}, u32[]{:S(2)}) %copy-start.2) | copy-done | bytes 280
  2.2 54.3 %shard_map.46 = f32[2,2,128,1024]{3,2,1,0:T(8,128)S(1)} custom-call(bf16[64,128,512]{2,1,0:T(8,128)(2,1)} %rec_hbm.1, bf16[80,512]{1,0:T(8,128)(2,1)S(1)} %copy-done, s32[4,64]{1,0:T(4,128)S(1)} %bitcast.2, s32[1,64]{1,0:T(1,128)S(1)} %bitcast.3), custom_call_target="tpu_custom_call" | custom-call | tf_op jit(solution)/shard_map/pallas_call | solution.py:397
  56.5 1.3 %copy.6 = f32[2,2,128,1024]{3,2,1,0:T(8,128)} copy(f32[2,2,128,1024]{3,2,1,0:T(8,128)S(1)} %shard_map.46) | data formatting | bytes 4194304
Async XLA Ops:
  0.0 0.9 %copy-start = (bf16[80,512]{1,0:T(8,128)(2,1)S(1)}, bf16[80,512]{1,0:T(8,128)(2,1)}, u32[]{:S(2)}) copy-start(bf16[80,512]{1,0:T(8,128)(2,1)} %constant.4.table_ref) | copy-start | bytes 245764
  0.9 0.7 %copy-start.1 = (s32[64,4]{0,1:T(4,128)S(1)}, s32[64,4]{0,1:T(4,128)}, u32[]{:S(2)}) copy-start(s32[64,4]{0,1:T(4,128)} %param.5) | copy-start | bytes 3076
  1.6 0.7 %copy-start.2 = (s32[64]{0:T(128)S(1)}, s32[64]{0:T(128)}, u32[]{:S(2)}) copy-start(s32[64]{0:T(128)} %param.6) | copy-start | bytes 772

commit v4 on v3

--- a/solution.py
+++ b/solution.py
@@ -19,8 +19,10 @@
 LEN = 512
 ROWS = 256
 SIDE = 128
-STEP = 4
+STEP = 8
 SLOTS = 40
+NEAR = (0, 1, 3, 2)
+OWNERS = (0, 1, 3, 2)
 NT = (((1,), (1,)), ((), ()))
 TN = (((0,), (0,)), ((), ()))
 QUARTERS = tuple(("q", q) for q in range(CHUNKS))
@@ -54,17 +56,18 @@
 
 
 def kernel(
-    rec_hbm, table_ref, flag_ref, mask_ref, out_ref,
-    rec, kept, square, word_ref, usable, stage_re, stage_im, spec, gathered, turned, block,
+    rec_hbm, table_hbm, flag_hbm, mask_hbm, out_hbm,
+    rec, table_ref, flag_ref, mask_ref, out_ref, kept, square, word_ref, usable, stage_re, stage_im, spec, gathered, turned, block,
     ring_words, all_words, flat_words, bits, inverse, side_out, side_in, mirror_out, mirror_in,
     side_scale_out, side_scale_in, mirror_scale_out, mirror_scale_in,
-    rec_sem, plane_send, plane_recv, wring_send, wring_recv, wplane_send, wplane_recv,
+    rec_sem, small_sem, out_sem, plane_send, plane_recv, wring_send, wring_recv, wplane_send, wplane_recv,
     up_send, up_recv, down_send, down_recv, side_send, side_recv, mirror_send, mirror_recv,
 ):
     tm = lax.axis_index("tm")
     freq = lax.axis_index("freq")
     y, zl = tm // 2, tm % 2
     mine = 2 * freq + zl
+    x, spot = mine // 8, mine % 8
 
     def plane_device(other):
         return (2 * y + other % 2, other // 2)
@@ -75,12 +78,19 @@
     def cross_device(offset):
         return (2 * ((y + offset) % Y) + 1 - zl, freq)
 
-    loads = []
-    for q in range(CHUNKS):
-        copy = pltpu.make_async_copy(
+    small = [
+        pltpu.make_async_copy(source, target, small_sem.at[n])
+        for n, (source, target) in enumerate(
+            ((flag_hbm, flag_ref), (mask_hbm, mask_ref), (table_hbm, table_ref)))
+    ]
+    loads = [
+        pltpu.make_async_copy(
             rec_hbm.at[pl.ds(PART * q, PART)], rec.at[pl.ds(PART * q, PART)], rec_sem.at[q])
+        for q in range(CHUNKS)
+    ]
+    for copy in small:
         copy.start()
-        loads.append(copy)
+    loads[0].start()
 
     barrier = pltpu.get_barrier_semaphore()
 
@@ -95,6 +105,8 @@
     for offset in (1, Y - 1):
         pl.semaphore_signal(barrier, inc=1, device_id=cross_device(offset), device_id_type=MESH)
 
+    for copy in small:
+        copy.wait()
     kept[...] = jnp.zeros_like(kept)
     kept[0:4, 0:STA] = flag_ref[...] * mask_ref[...]
     square[...] = jnp.zeros_like(square)
@@ -157,28 +169,31 @@
             plane_send.at[q, receiver], plane_recv.at[q, sender],
             device_id=plane_device(receiver), device_id_type=MESH)
 
+    def group_peer(step, j):
+        return 8 * ((x + step) % 4) + (spot + j) % 8
+
     def send_plane(q):
-        def one(offset, carry):
-            plane_copy(q, mine, (mine + offset) % PLANE).start()
+        for step in NEAR:
+            def one(j, carry):
+                plane_copy(q, mine, group_peer(step, j)).start()
+                return carry
+
+            lax.fori_loop(0 if step else 1, 8, one, 0)
+        gathered[y, zl, freq, PART * q : PART * (q + 1), :] = spec[mine, PART * q : PART * (q + 1), :]
+
+    def from_plane(q, step):
+        def one(j, carry):
+            sender = group_peer(step, j)
+            plane_copy(q, sender, (sender + 1) % PLANE).wait_recv()
             return carry
 
-        lax.fori_loop(1, PLANE, one, 0)
-        gathered[y, zl, freq, PART * q : PART * (q + 1), :] = spec[mine, PART * q : PART * (q + 1), :]
-
-    def from_plane(q, shift):
-        def one(i, carry):
-            sender = 8 * ((y + shift) % Y) + i
-
-            @pl.when(sender != mine)
-            def _():
-                plane_copy(q, sender, (sender + 1) % PLANE).wait_recv()
-
-            return carry
-
-        lax.fori_loop(0, 8, one, 0)
+        lax.fori_loop(0 if step else 1, 8, one, 0)
 
     for q in range(CHUNKS):
         loads[q].wait()
+        if q == 0:
+            for copy in loads[1:]:
+                copy.start()
         transform(q)
         if q == 0:
             pl.semaphore_wait(barrier, PLANE - 1 + Y - 1 + 2)
@@ -209,15 +224,30 @@
     ups = [message(entry, slot, 1, up_send, up_recv) for slot, entry in enumerate(UP)]
     downs = [message(entry, slot, -1, down_send, down_recv) for slot, entry in enumerate(DOWN)]
 
+    def ring_start(q, step):
+        group = (x + step) % 4
+        shift = (group - y + Y) % Y
+        ref = gathered.at[y, :, pl.ds(4 * group, 4), pl.ds(PART * q, PART), :]
+        upward = (shift + 1) // 2 == 1
+
+        @pl.when(upward)
+        def _():
+            slot = CHUNKS * (shift - 1) + q
+            pltpu.make_async_remote_copy(
+                ref, ref, up_send.at[slot], up_recv.at[slot],
+                device_id=ring_device(1), device_id_type=MESH).start()
+
+        @pl.when(jnp.logical_not(upward))
+        def _():
+            slot = CHUNKS * ((3 - shift) // 3) + q
+            pltpu.make_async_remote_copy(
+                ref, ref, down_send.at[slot], down_recv.at[slot],
+                device_id=ring_device(Y - 1), device_id_type=MESH).start()
+
     for q in range(CHUNKS):
-        from_plane(q, 1)
-        ups[q].start()
-        from_plane(q, 3)
-        downs[q].start()
-        from_plane(q, 2)
-        ups[4 + q].start()
-        from_plane(q, 0)
-        downs[4 + q].start()
+        for step in NEAR:
+            from_plane(q, step)
+            ring_start(q, step)
         if q == 0:
             for copy in word_ring:
                 copy.wait()
@@ -288,14 +318,24 @@
     def decode(codes, scale):
         return codes.astype(jnp.int32).astype(jnp.float32) * scale
 
-    def multiply(shift, half=None):
+    def multiply(shift, half=None, late=None):
         count = 4 if half is None else 2
         width = STA * count
         group = 4 * ((y + shift) % Y) + (0 if half is None else 2 * half)
-        right = jnp.concatenate(
-            [gathered[owner, part, pl.ds(group, count)].reshape(width, 2 * WIN)
-             for owner in range(Y) for part in range(2)], axis=1)
-        both = lax.dot_general(turned[...], right, NT, preferred_element_type=jnp.float32)
+
+        def product(first, last):
+            right = jnp.concatenate(
+                [gathered[(y + k) % Y, part, pl.ds(group, count)].reshape(width, 2 * WIN)
+                 for k in OWNERS[first:last] for part in range(2)], axis=1)
+            return lax.dot_general(
+                turned[:, 512 * first : 512 * last], right, NT, preferred_element_type=jnp.float32)
+
+        if late is None:
+            both = product(0, 4)
+        else:
+            both = product(0, 3)
+            late.wait_recv()
+            both = both + product(3, 4)
         at = slice(SIDE, ROWS) if half == 1 else slice(0, width)
         slot = shift if half is None else shift + half
         col = pl.multiple_of(group * STA, SIDE)
@@ -321,10 +361,10 @@
         ups[q].wait_recv()
         ups[8 + q].wait_recv()
         downs[8 + q].wait_recv()
-    for owner in range(Y):
+    for n, k in enumerate(OWNERS):
         for part in range(2):
-            left = gathered[owner, part, pl.ds(4 * y, 4)].reshape(ROWS, 2 * WIN)
-            at = (2 * owner + part) * 256
+            left = gathered[(y + k) % Y, part, pl.ds(4 * y, 4)].reshape(ROWS, 2 * WIN)
+            at = (2 * n + part) * 256
             turned[0:ROWS, at : at + 256] = left
             turned[ROWS : 2 * ROWS, at : at + 256] = jnp.concatenate(
                 [left[:, WIN:], -left[:, :WIN]], axis=1)
@@ -348,12 +388,40 @@
     sides.append(multiply(0))
     ups[12].wait_recv()
     downs[12].wait_recv()
-    downs[13].wait_recv()
-    sides.append(multiply(2, 0))
+    sides.append(multiply(2, 0, downs[13]))
     ups[13].wait_recv()
     downs[14].wait_recv()
-    downs[15].wait_recv()
-    sides.append(multiply(2, 1))
+    sides.append(multiply(2, 1, downs[15]))
+
+    def column(shift, half=None):
+        if half is None:
+            return pl.ds(pl.multiple_of(((y + shift) % Y) * ROWS, ROWS), ROWS)
+        return pl.ds(pl.multiple_of(((y + shift) % Y) * ROWS + SIDE * half, SIDE), SIDE)
+
+    stores = []
+
+    def store(which, columns):
+        copy = pltpu.make_async_copy(
+            out_ref.at[which, :, :, columns], out_hbm.at[which, :, :, columns], out_sem.at[len(stores)])
+        copy.start()
+        stores.append(copy)
+
+    for shift in range(3):
+        store(zl, column(shift))
+    for shift in (1, 0):
+        for copy in sides[1 - shift]:
+            copy.wait()
+        for plane in range(2):
+            out_ref[1 - zl, plane, :, column(shift)] = decode(
+                side_in[shift, plane], side_scale_in[shift, plane : plane + 1])
+        store(1 - zl, column(shift))
+    for copy in mirrors:
+        copy.wait()
+    for n in range(2):
+        for plane in range(2):
+            out_ref[n, plane, :, column(3)] = decode(
+                mirror_in[n, plane], mirror_scale_in[n, plane : plane + 1])
+        store(n, column(3))
 
     def sent(offset, carry):
         other = (mine + offset) % PLANE
@@ -365,42 +433,32 @@
     lax.fori_loop(1, PLANE, sent, 0)
     for copy in ups + downs:
         copy.wait_send()
-
-    def column(shift):
-        return pl.ds(pl.multiple_of(((y + shift) % Y) * ROWS, ROWS), ROWS)
-
-    for shift in (1, 0):
-        for copy in sides[1 - shift]:
-            copy.wait()
-        for plane in range(2):
-            out_ref[1 - zl, plane, :, column(shift)] = decode(
-                side_in[shift, plane], side_scale_in[shift, plane : plane + 1])
-    for copy in mirrors:
-        copy.wait()
-    for n in range(2):
-        for plane in range(2):
-            out_ref[n, plane, :, column(3)] = decode(
-                mirror_in[n, plane], mirror_scale_in[n, plane : plane + 1])
     for half in range(2):
         for copy in sides[2 + half]:
             copy.wait()
-        at = slice(SIDE * half, SIDE * (half + 1))
-        col = pl.multiple_of(((y + 2) % Y) * ROWS + SIDE * half, SIDE)
         for plane in range(2):
-            out_ref[1 - zl, plane, :, pl.ds(col, SIDE)] = decode(
-                side_in[2, plane, :, at], side_scale_in[2 + half, plane : plane + 1, 0:SIDE])
+            out_ref[1 - zl, plane, :, column(2, half)] = decode(
+                side_in[2, plane, :, SIDE * half : SIDE * (half + 1)],
+                side_scale_in[2 + half, plane : plane + 1, 0:SIDE])
+        store(1 - zl, column(2, half))
+    for copy in stores:
+        copy.wait()
 
 
 def stack_up(records, table, flags, mask):
     dma = pltpu.SemaphoreType.DMA
-    vmem = pl.BlockSpec(memory_space=pltpu.VMEM)
+    anywhere = pl.BlockSpec(memory_space=pl.ANY)
     return pl.pallas_call(
         kernel,
         out_shape=jax.ShapeDtypeStruct((2, 2, SIDE, 1024), jnp.float32),
-        in_specs=[pl.BlockSpec(memory_space=pltpu.HBM), vmem, vmem, vmem],
-        out_specs=vmem,
+        in_specs=[anywhere] * 4,
+        out_specs=anywhere,
         scratch_shapes=[
             pltpu.VMEM((STA, WIN, LEN), jnp.bfloat16),
+            pltpu.VMEM((2 * SLOTS, LEN), jnp.bfloat16),
+            pltpu.VMEM((4, STA), jnp.int32),
+            pltpu.VMEM((1, STA), jnp.int32),
+            pltpu.VMEM((2, 2, SIDE, 1024), jnp.float32),
             pltpu.VMEM((8, WIN), jnp.int32),
             pltpu.VMEM((WIN, WIN), jnp.int32),
             pltpu.VMEM((2, WIN), jnp.int32),
@@ -424,13 +482,13 @@
             pltpu.VMEM((4, 2, ROWS), jnp.float32),
             pltpu.VMEM((2, 2, ROWS), jnp.float32),
             pltpu.VMEM((2, 2, ROWS), jnp.float32),
-            dma((CHUNKS,)), dma((CHUNKS, PLANE)), dma((CHUNKS, PLANE)),
+            dma((CHUNKS,)), dma((3,)), dma((9,)), dma((CHUNKS, PLANE)), dma((CHUNKS, PLANE)),
             dma((Y,)), dma((Y,)), dma((PLANE,)), dma((PLANE,)),
             dma((len(UP),)), dma((len(UP),)), dma((len(DOWN),)), dma((len(DOWN),)),
             dma((2, 4)), dma((2, 4)), dma((2, 2)), dma((2, 2)),
         ],
         compiler_params=pltpu.CompilerParams(
-            collective_id=0, has_side_effects=True, vmem_limit_bytes=48 << 20),
+            collective_id=0, has_side_effects=True, vmem_limit_bytes=60 << 20),
     )(records, table, flags, mask)
 
 

time: 58 us -> 57.5 us (level)
    unnamed x7 -> x1, local copies, waits for them, and re-layouts: 3.54 us -> 3.16 us
where the time goes in v4:
time: 57.5 us; the launch traced here: 57.3 us
  Pallas kernels  54.2 us (94%)
  local copies, waits for them, and re-layouts  3.16 us (5%)
    pallas_call x1, Pallas kernels, stack_up(): pl.pallas_call(kernel, out_shape=jax.ShapeDtypeStruct((2, 2, SIDE, 1024),...  54.2 us
    unnamed x1, local copies, waits for them, and re-layouts  3.16 us

profile of v4, /device:TPU:0, one launch (start us, length us, event | category | flops | bytes accessed | tf_op | source)
XLA Modules:
  0.0 57.3 jit_solution(6496974984545864179)
XLA Ops:
  0.0 54.2 %shard_map.46 = f32[2,2,128,1024]{3,2,1,0:T(8,128)} custom-call(bf16[64,128,512]{2,1,0:T(8,128)(2,1)} %rec_hbm.1, bf16[80,512]{1,0:T(8,128)(2,1)} %constant.4.table_hbm, s32[4,64]{1,0:T(4,128)} %bitcast.2, s32[1,64]{1,0:T(1,128)} %bitcast.3), custom_call_target="tpu_custom_call" | custom-call | tf_op jit(solution)/shard_map/pallas_call | solution.py:451
  54.2 3.2 %copy.6 = f32[2,2,128,1024]{3,2,1,0:T(8,128)} copy(f32[2,2,128,1024]{3,2,1,0:T(8,128)} %shard_map.46) | data formatting | bytes 4194304

commit v5 on v4

--- a/solution.py
+++ b/solution.py
@@ -2,7 +2,6 @@
 
 import jax
 import jax.numpy as jnp
-import numpy as np
 from jax import lax
 from jax.experimental import pallas as pl
 from jax.experimental.pallas import tpu as pltpu
@@ -41,26 +40,35 @@
 )
 
 
+def turn(phase):
+    quarter = (phase + 64) // 128
+    a = (phase - 128 * quarter).astype(jnp.float32) * (2.0 * math.pi / LEN)
+    b = a * a
+    c = 1.0 + b * (-0.5 + b * (1.0 / 24 + b * (-1.0 / 720 + b * (1.0 / 40320))))
+    s = a * (1.0 + b * (-1.0 / 6 + b * (1.0 / 120 + b * (-1.0 / 5040 + b * (1.0 / 362880)))))
+    odd = quarter % 2 == 1
+    cosine = jnp.where(odd, s, c)
+    sine = jnp.where(odd, c, s)
+    cosine = jnp.where((quarter == 1) | (quarter == 2), -cosine, cosine)
+    sine = jnp.where((quarter == 2) | (quarter == 3), -sine, sine)
+    return cosine, sine
+
+
 def transform_table():
-    t = np.arange(LEN)
-    taper = (0.5 - 0.5 * np.cos(2.0 * math.pi * t / LEN)) / math.sqrt(LEN)
-    table = np.zeros((2, 5, 8, LEN))
-    for v in range(5):
-        for i in range(8):
-            b = 5 * i + v
-            if b < 36:
-                angle = 2.0 * math.pi * ((b * t) % LEN) / LEN
-                table[0, v, i] = np.cos(angle) * taper
-                table[1, v, i] = -np.sin(angle) * taper
-    return jnp.asarray(table.reshape(2 * SLOTS, LEN).astype(np.float32)).astype(jnp.bfloat16)
+    row = lax.broadcasted_iota(jnp.int32, (SLOTS, LEN), 0)
+    t = lax.broadcasted_iota(jnp.int32, (SLOTS, LEN), 1)
+    b = 5 * (row % 8) + row // 8
+    taper = jnp.where(b < 36, (0.5 - 0.5 * turn(t)[0]) * (1.0 / math.sqrt(LEN)), 0.0)
+    cosine, sine = turn((b * t) % LEN)
+    return jnp.concatenate([cosine * taper, -sine * taper], axis=0).astype(jnp.bfloat16)
 
 
 def kernel(
-    rec_hbm, table_hbm, flag_hbm, mask_hbm, out_hbm,
-    rec, table_ref, flag_ref, mask_ref, out_ref, kept, square, word_ref, usable, stage_re, stage_im, spec, gathered, turned, block,
+    rec_hbm, flag_ref, out_ref,
+    rec, table_ref, kept, square, word_ref, usable, stage_re, stage_im, spec, gathered, turned, block,
     ring_words, all_words, flat_words, bits, inverse, side_out, side_in, mirror_out, mirror_in,
     side_scale_out, side_scale_in, mirror_scale_out, mirror_scale_in,
-    rec_sem, small_sem, out_sem, plane_send, plane_recv, wring_send, wring_recv, wplane_send, wplane_recv,
+    rec_sem, plane_send, plane_recv, wring_send, wring_recv, wplane_send, wplane_recv,
     up_send, up_recv, down_send, down_recv, side_send, side_recv, mirror_send, mirror_recv,
 ):
     tm = lax.axis_index("tm")
@@ -78,18 +86,11 @@
     def cross_device(offset):
         return (2 * ((y + offset) % Y) + 1 - zl, freq)
 
-    small = [
-        pltpu.make_async_copy(source, target, small_sem.at[n])
-        for n, (source, target) in enumerate(
-            ((flag_hbm, flag_ref), (mask_hbm, mask_ref), (table_hbm, table_ref)))
-    ]
     loads = [
         pltpu.make_async_copy(
             rec_hbm.at[pl.ds(PART * q, PART)], rec.at[pl.ds(PART * q, PART)], rec_sem.at[q])
         for q in range(CHUNKS)
     ]
-    for copy in small:
-        copy.start()
     loads[0].start()
 
     barrier = pltpu.get_barrier_semaphore()
@@ -105,10 +106,9 @@
     for offset in (1, Y - 1):
         pl.semaphore_signal(barrier, inc=1, device_id=cross_device(offset), device_id_type=MESH)
 
-    for copy in small:
-        copy.wait()
+    table_ref[...] = transform_table()
     kept[...] = jnp.zeros_like(kept)
-    kept[0:4, 0:STA] = flag_ref[...] * mask_ref[...]
+    kept[0:4, 0:STA] = flag_ref[...]
     square[...] = jnp.zeros_like(square)
     square[0:8, :] = kept[...]
     words = jnp.transpose(square[...])[0:STA]
@@ -318,29 +318,7 @@
     def decode(codes, scale):
         return codes.astype(jnp.int32).astype(jnp.float32) * scale
 
-    def multiply(shift, half=None, late=None):
-        count = 4 if half is None else 2
-        width = STA * count
-        group = 4 * ((y + shift) % Y) + (0 if half is None else 2 * half)
-
-        def product(first, last):
-            right = jnp.concatenate(
-                [gathered[(y + k) % Y, part, pl.ds(group, count)].reshape(width, 2 * WIN)
-                 for k in OWNERS[first:last] for part in range(2)], axis=1)
-            return lax.dot_general(
-                turned[:, 512 * first : 512 * last], right, NT, preferred_element_type=jnp.float32)
-
-        if late is None:
-            both = product(0, 4)
-        else:
-            both = product(0, 3)
-            late.wait_recv()
-            both = both + product(3, 4)
-        at = slice(SIDE, ROWS) if half == 1 else slice(0, width)
-        slot = shift if half is None else shift + half
-        col = pl.multiple_of(group * STA, SIDE)
-        scale = inverse[:, pl.ds(col, width)]
-        block[shift, :, :, at] = both.reshape(2, ROWS, width) * scale
+    def swap(shift, slot, at, width):
         for plane in range(2):
             side_out[shift, plane, :, at], side_scale_out[slot, plane : plane + 1, 0:width] = encode(
                 block[shift, plane, pl.ds(away_at, SIDE), at])
@@ -354,7 +332,45 @@
         ]
         for copy in copies:
             copy.start()
-        out_ref[zl, :, :, pl.ds(col, width)] = block[shift, :, pl.ds(kept_at, SIDE), at]
+        return copies
+
+    def right_side(group, count, first, last):
+        return jnp.concatenate(
+            [gathered[(y + k) % Y, part, pl.ds(group, count)].reshape(STA * count, 2 * WIN)
+             for k in OWNERS[first:last] for part in range(2)], axis=1)
+
+    def multiply(shift):
+        both = lax.dot_general(
+            turned[...], right_side(4 * ((y + shift) % Y), 4, 0, 4), NT,
+            preferred_element_type=jnp.float32)
+        col = pl.multiple_of(((y + shift) % Y) * ROWS, ROWS)
+        block[shift] = both.reshape(2, ROWS, ROWS) * inverse[:, pl.ds(col, ROWS)]
+        copies = swap(shift, shift, slice(0, ROWS), ROWS)
+        out_ref[zl, :, :, pl.ds(col, ROWS)] = block[shift, :, pl.ds(kept_at, SIDE), :]
+        return copies
+
+    def multiply_late(half, late):
+        group = 4 * ((y + 2) % Y) + 2 * half
+        at = slice(SIDE * half, SIDE * (half + 1))
+        col = pl.multiple_of(group * STA, SIDE)
+        early = lax.dot_general(
+            turned[:, 0:1536], right_side(group, 2, 0, 3), NT, preferred_element_type=jnp.float32)
+        block[2, :, :, at] = early.reshape(2, ROWS, SIDE)
+        late.wait_recv()
+        right = right_side(group, 2, 3, 4)
+
+        def finish(rows):
+            left = jnp.concatenate(
+                [turned[pl.ds(rows + start, SIDE), 1536:2048] for start in (0, ROWS)], axis=0)
+            both = lax.dot_general(left, right, NT, preferred_element_type=jnp.float32)
+            block[2, :, pl.ds(rows, SIDE), at] = (
+                block[2, :, pl.ds(rows, SIDE), at] + both.reshape(2, SIDE, SIDE)
+            ) * inverse[pl.ds(rows, SIDE), pl.ds(col, SIDE)]
+
+        finish(away_at)
+        copies = swap(2, 2 + half, at, SIDE)
+        finish(kept_at)
+        out_ref[zl, :, :, pl.ds(col, SIDE)] = block[2, :, pl.ds(kept_at, SIDE), at]
         return copies
 
     for q in range(CHUNKS):
@@ -388,40 +404,28 @@
     sides.append(multiply(0))
     ups[12].wait_recv()
     downs[12].wait_recv()
-    sides.append(multiply(2, 0, downs[13]))
+    sides.append(multiply_late(0, downs[13]))
     ups[13].wait_recv()
     downs[14].wait_recv()
-    sides.append(multiply(2, 1, downs[15]))
+    sides.append(multiply_late(1, downs[15]))
 
     def column(shift, half=None):
         if half is None:
             return pl.ds(pl.multiple_of(((y + shift) % Y) * ROWS, ROWS), ROWS)
         return pl.ds(pl.multiple_of(((y + shift) % Y) * ROWS + SIDE * half, SIDE), SIDE)
 
-    stores = []
-
-    def store(which, columns):
-        copy = pltpu.make_async_copy(
-            out_ref.at[which, :, :, columns], out_hbm.at[which, :, :, columns], out_sem.at[len(stores)])
-        copy.start()
-        stores.append(copy)
-
-    for shift in range(3):
-        store(zl, column(shift))
     for shift in (1, 0):
         for copy in sides[1 - shift]:
             copy.wait()
         for plane in range(2):
             out_ref[1 - zl, plane, :, column(shift)] = decode(
                 side_in[shift, plane], side_scale_in[shift, plane : plane + 1])
-        store(1 - zl, column(shift))
     for copy in mirrors:
         copy.wait()
     for n in range(2):
         for plane in range(2):
             out_ref[n, plane, :, column(3)] = decode(
                 mirror_in[n, plane], mirror_scale_in[n, plane : plane + 1])
-        store(n, column(3))
 
     def sent(offset, carry):
         other = (mine + offset) % PLANE
@@ -440,25 +444,19 @@
             out_ref[1 - zl, plane, :, column(2, half)] = decode(
                 side_in[2, plane, :, SIDE * half : SIDE * (half + 1)],
                 side_scale_in[2 + half, plane : plane + 1, 0:SIDE])
-        store(1 - zl, column(2, half))
-    for copy in stores:
-        copy.wait()
-
-
-def stack_up(records, table, flags, mask):
+
+
+def stack_up(records, flags):
     dma = pltpu.SemaphoreType.DMA
-    anywhere = pl.BlockSpec(memory_space=pl.ANY)
+    vmem = pl.BlockSpec(memory_space=pltpu.VMEM)
     return pl.pallas_call(
         kernel,
         out_shape=jax.ShapeDtypeStruct((2, 2, SIDE, 1024), jnp.float32),
-        in_specs=[anywhere] * 4,
-        out_specs=anywhere,
+        in_specs=[pl.BlockSpec(memory_space=pl.ANY), vmem],
+        out_specs=vmem,
         scratch_shapes=[
             pltpu.VMEM((STA, WIN, LEN), jnp.bfloat16),
             pltpu.VMEM((2 * SLOTS, LEN), jnp.bfloat16),
-            pltpu.VMEM((4, STA), jnp.int32),
-            pltpu.VMEM((1, STA), jnp.int32),
-            pltpu.VMEM((2, 2, SIDE, 1024), jnp.float32),
             pltpu.VMEM((8, WIN), jnp.int32),
             pltpu.VMEM((WIN, WIN), jnp.int32),
             pltpu.VMEM((2, WIN), jnp.int32),
@@ -482,18 +480,18 @@
             pltpu.VMEM((4, 2, ROWS), jnp.float32),
             pltpu.VMEM((2, 2, ROWS), jnp.float32),
             pltpu.VMEM((2, 2, ROWS), jnp.float32),
-            dma((CHUNKS,)), dma((3,)), dma((9,)), dma((CHUNKS, PLANE)), dma((CHUNKS, PLANE)),
+            dma((CHUNKS,)), dma((CHUNKS, PLANE)), dma((CHUNKS, PLANE)),
             dma((Y,)), dma((Y,)), dma((PLANE,)), dma((PLANE,)),
             dma((len(UP),)), dma((len(UP),)), dma((len(DOWN),)), dma((len(DOWN),)),
             dma((2, 4)), dma((2, 4)), dma((2, 2)), dma((2, 2)),
         ],
         compiler_params=pltpu.CompilerParams(
-            collective_id=0, has_side_effects=True, vmem_limit_bytes=60 << 20),
-    )(records, table, flags, mask)
+            collective_id=0, has_side_effects=True, vmem_limit_bytes=48 << 20),
+    )(records, flags)
 
 
 def local(records, gap_flags, station_mask):
-    return stack_up(records, transform_table(), gap_flags.T, station_mask[None])
+    return stack_up(records, gap_flags.T * station_mask[None])
 
 
 def solution(mesh):

time: 57.5 us -> 55.5 us (0.965)
  local copies, waits for them, and re-layouts: 3.16 us -> 1.32 us
  Pallas kernels: 54.2 us -> 53.3 us
  other arithmetic: 0 us -> 0.69 us
    unnamed x1, local copies, waits for them, and re-layouts: 3.16 us -> 1.32 us
    pallas_call x1, Pallas kernels: 54.2 us -> 53.3 us  [stack_up(): pl.pallas_call(kernel, out_shape=jax.ShapeDtypeStruct((2, 2, SIDE, 1024),...]
    mul x0 -> x1, other arithmetic: none -> 0.69 us  [local(): return stack_up(records, gap_flags.T * station_mask[None])]
where the time goes in v5:
time: 55.5 us; the launch traced here: 55.3 us
  Pallas kernels  53.3 us (96%)
  local copies, waits for them, and re-layouts  1.32 us (2%)
  other arithmetic  0.69 us (1%)
    pallas_call x1, Pallas kernels, stack_up(): pl.pallas_call(kernel, out_shape=jax.ShapeDtypeStruct((2, 2, SIDE, 1024),...  53.3 us
    unnamed x1, local copies, waits for them, and re-layouts  1.32 us

profile of v5, /device:TPU:0, one launch (start us, length us, event | category | flops | bytes accessed | tf_op | source)
XLA Modules:
  0.0 55.3 jit_solution(16793781422160158736)
XLA Ops:
  0.0 0.7 %multiply_bitcast_fusion.flag_ref = s32[4,64]{1,0:T(4,128)S(1)} fusion(s32[64,4]{0,1:T(4,128)} %param.4, s32[64]{0:T(128)} %param.5), kind=kLoop, calls=%fused_computation | loop fusion | flops 256 | bytes 2304 | tf_op jit(solution)/shard_map/mul | solution.py:494
  0.7 53.3 %shard_map.37 = f32[2,2,128,1024]{3,2,1,0:T(8,128)S(1)} custom-call(bf16[64,128,512]{2,1,0:T(8,128)(2,1)} %rec_hbm.1, s32[4,64]{1,0:T(4,128)S(1)} %multiply_bitcast_fusion.flag_ref), custom_call_target="tpu_custom_call" | custom-call | tf_op jit(solution)/shard_map/pallas_call | solution.py:452
  54.0 1.3 %copy.5 = f32[2,2,128,1024]{3,2,1,0:T(8,128)} copy(f32[2,2,128,1024]{3,2,1,0:T(8,128)S(1)} %shard_map.37) | data formatting | bytes 4194304

commit v6 on v5

--- a/solution.py
+++ b/solution.py
@@ -100,7 +100,8 @@
             barrier, inc=1, device_id=plane_device((mine + offset) % PLANE), device_id_type=MESH)
         return carry
 
-    lax.fori_loop(1, PLANE, greet, 0)
+    for offset in range(1, PLANE):
+        greet(offset, 0)
     for offset in range(1, Y):
         pl.semaphore_signal(barrier, inc=1, device_id=ring_device(offset), device_id_type=MESH)
     for offset in (1, Y - 1):
@@ -174,20 +175,14 @@
 
     def send_plane(q):
         for step in NEAR:
-            def one(j, carry):
+            for j in range(0 if step else 1, 8):
                 plane_copy(q, mine, group_peer(step, j)).start()
-                return carry
-
-            lax.fori_loop(0 if step else 1, 8, one, 0)
         gathered[y, zl, freq, PART * q : PART * (q + 1), :] = spec[mine, PART * q : PART * (q + 1), :]
 
     def from_plane(q, step):
-        def one(j, carry):
+        for j in range(0 if step else 1, 8):
             sender = group_peer(step, j)
             plane_copy(q, sender, (sender + 1) % PLANE).wait_recv()
-            return carry
-
-        lax.fori_loop(0 if step else 1, 8, one, 0)
 
     for q in range(CHUNKS):
         loads[q].wait()
@@ -272,6 +267,7 @@
         downs[8 + q].start()
     ups[12].start()
     downs[12].start()
+    ups[13].start()
     for q in range(CHUNKS):
         downs[4 + q].wait_recv()
     downs[13].start()
@@ -400,7 +396,6 @@
     ]
     for copy in mirrors:
         copy.start()
-    ups[13].start()
     sides.append(multiply(0))
     ups[12].wait_recv()
     downs[12].wait_recv()

time: 55.5 us -> 52.7 us (0.950)
  Pallas kernels: 53.3 us -> 50.2 us
    pallas_call x1, Pallas kernels: 53.3 us -> 50.2 us  [stack_up(): pl.pallas_call(kernel, out_shape=jax.ShapeDtypeStruct((2, 2, SIDE, 1024),...]
where the time goes in v6:
time: 52.7 us; the launch traced here: 52.2 us
  Pallas kernels  50.2 us (95%)
  local copies, waits for them, and re-layouts  1.32 us (3%)
  other arithmetic  0.69 us (1%)
    pallas_call x1, Pallas kernels, stack_up(): pl.pallas_call(kernel, out_shape=jax.ShapeDtypeStruct((2, 2, SIDE, 1024),...  50.2 us
    unnamed x1, local copies, waits for them, and re-layouts  1.32 us

profile of v6, /device:TPU:0, one launch (start us, length us, event | category | flops | bytes accessed | tf_op | source)
XLA Modules:
  0.0 52.2 jit_solution(8871684357708106583)
XLA Ops:
  0.0 0.7 %multiply_bitcast_fusion.flag_ref = s32[4,64]{1,0:T(4,128)S(1)} fusion(s32[64,4]{0,1:T(4,128)} %param.4, s32[64]{0:T(128)} %param.5), kind=kLoop, calls=%fused_computation | loop fusion | flops 256 | bytes 2304 | tf_op jit(solution)/shard_map/mul | solution.py:489
  0.7 50.2 %shard_map.37 = f32[2,2,128,1024]{3,2,1,0:T(8,128)S(1)} custom-call(bf16[64,128,512]{2,1,0:T(8,128)(2,1)} %rec_hbm.1, s32[4,64]{1,0:T(4,128)S(1)} %multiply_bitcast_fusion.flag_ref), custom_call_target="tpu_custom_call" | custom-call | tf_op jit(solution)/shard_map/pallas_call | solution.py:447
  50.8 1.3 %copy.5 = f32[2,2,128,1024]{3,2,1,0:T(8,128)} copy(f32[2,2,128,1024]{3,2,1,0:T(8,128)S(1)} %shard_map.37) | data formatting | bytes 4194304

commit v7 on v6

--- a/solution.py
+++ b/solution.py
@@ -337,10 +337,10 @@
 
     def multiply(shift):
         both = lax.dot_general(
-            turned[...], right_side(4 * ((y + shift) % Y), 4, 0, 4), NT,
+            turned[:, 1536:2048], right_side(4 * ((y + shift) % Y), 4, 3, 4), NT,
             preferred_element_type=jnp.float32)
         col = pl.multiple_of(((y + shift) % Y) * ROWS, ROWS)
-        block[shift] = both.reshape(2, ROWS, ROWS) * inverse[:, pl.ds(col, ROWS)]
+        block[shift] = (block[shift] + both.reshape(2, ROWS, ROWS)) * inverse[:, pl.ds(col, ROWS)]
         copies = swap(shift, shift, slice(0, ROWS), ROWS)
         out_ref[zl, :, :, pl.ds(col, ROWS)] = block[shift, :, pl.ds(kept_at, SIDE), :]
         return copies
@@ -369,18 +369,28 @@
         out_ref[zl, :, :, pl.ds(col, SIDE)] = block[2, :, pl.ds(kept_at, SIDE), at]
         return copies
 
-    for q in range(CHUNKS):
-        ups[q].wait_recv()
-        ups[8 + q].wait_recv()
-        downs[8 + q].wait_recv()
-    for n, k in enumerate(OWNERS):
+    def left_side(n):
         for part in range(2):
-            left = gathered[(y + k) % Y, part, pl.ds(4 * y, 4)].reshape(ROWS, 2 * WIN)
+            left = gathered[(y + OWNERS[n]) % Y, part, pl.ds(4 * y, 4)].reshape(ROWS, 2 * WIN)
             at = (2 * n + part) * 256
             turned[0:ROWS, at : at + 256] = left
             turned[ROWS : 2 * ROWS, at : at + 256] = jnp.concatenate(
                 [left[:, WIN:], -left[:, :WIN]], axis=1)
-    sides = [multiply(1)]
+
+    for q in range(CHUNKS):
+        ups[q].wait_recv()
+    for n in range(3):
+        left_side(n)
+    for shift in (1, 0):
+        early = lax.dot_general(
+            turned[:, 0:1536], right_side(4 * ((y + shift) % Y), 4, 0, 3), NT,
+            preferred_element_type=jnp.float32)
+        block[shift] = early.reshape(2, ROWS, ROWS)
+    for q in range(CHUNKS):
+        ups[8 + q].wait_recv()
+        downs[8 + q].wait_recv()
+    left_side(3)
+    sides = [multiply(1), multiply(0)]
     for plane, sign in ((0, 1.0), (1, -1.0)):
         flipped = sign * jnp.transpose(block[1, plane])
         for h in range(2):
@@ -396,7 +406,6 @@
     ]
     for copy in mirrors:
         copy.start()
-    sides.append(multiply(0))
     ups[12].wait_recv()
     downs[12].wait_recv()
     sides.append(multiply_late(0, downs[13]))

time: 52.7 us -> 51.9 us (0.985)
  Pallas kernels: 50.2 us -> 49.5 us
    pallas_call x1, Pallas kernels: 50.2 us -> 49.5 us  [stack_up(): pl.pallas_call(kernel, out_shape=jax.ShapeDtypeStruct((2, 2, SIDE, 1024),...]
where the time goes in v7:
time: 51.9 us; the launch traced here: 51.5 us
  Pallas kernels  49.5 us (95%)
  local copies, waits for them, and re-layouts  1.32 us (3%)
  other arithmetic  0.69 us (1%)
    pallas_call x1, Pallas kernels, stack_up(): pl.pallas_call(kernel, out_shape=jax.ShapeDtypeStruct((2, 2, SIDE, 1024),...  49.5 us
    unnamed x1, local copies, waits for them, and re-layouts  1.32 us

profile of v7, /device:TPU:0, one launch (start us, length us, event | category | flops | bytes accessed | tf_op | source)
XLA Modules:
  0.0 51.5 jit_solution(9528795443374048631)
XLA Ops:
  0.0 0.7 %multiply_bitcast_fusion.flag_ref = s32[4,64]{1,0:T(4,128)S(1)} fusion(s32[64,4]{0,1:T(4,128)} %param.4, s32[64]{0:T(128)} %param.5), kind=kLoop, calls=%fused_computation | loop fusion | flops 256 | bytes 2304 | tf_op jit(solution)/shard_map/mul | solution.py:498
  0.7 49.5 %shard_map.37 = f32[2,2,128,1024]{3,2,1,0:T(8,128)S(1)} custom-call(bf16[64,128,512]{2,1,0:T(8,128)(2,1)} %rec_hbm.1, s32[4,64]{1,0:T(4,128)S(1)} %multiply_bitcast_fusion.flag_ref), custom_call_target="tpu_custom_call" | custom-call | tf_op jit(solution)/shard_map/pallas_call | solution.py:456
  50.2 1.3 %copy.5 = f32[2,2,128,1024]{3,2,1,0:T(8,128)} copy(f32[2,2,128,1024]{3,2,1,0:T(8,128)S(1)} %shard_map.37) | data formatting | bytes 4194304

commit v8 on v7

--- a/solution.py
+++ b/solution.py
@@ -314,6 +314,15 @@
     def decode(codes, scale):
         return codes.astype(jnp.int32).astype(jnp.float32) * scale
 
+    def side_copy(source, target, kind, slot):
+        return pltpu.make_async_remote_copy(
+            source, target, side_send.at[kind, slot], side_recv.at[kind, slot],
+            device_id=(2 * y + 1 - zl, freq), device_id_type=MESH)
+
+    def start(pairs, slot):
+        for kind in range(0 if len(pairs) == 1 else 1, len(pairs)):
+            side_copy(*pairs[kind], kind, slot).start()
+
     def swap(shift, slot, at, width):
         for plane in range(2):
             side_out[shift, plane, :, at], side_scale_out[slot, plane : plane + 1, 0:width] = encode(
@@ -355,19 +364,26 @@
         late.wait_recv()
         right = right_side(group, 2, 3, 4)
 
-        def finish(rows):
-            left = jnp.concatenate(
-                [turned[pl.ds(rows + start, SIDE), 1536:2048] for start in (0, ROWS)], axis=0)
-            both = lax.dot_general(left, right, NT, preferred_element_type=jnp.float32)
-            block[2, :, pl.ds(rows, SIDE), at] = (
-                block[2, :, pl.ds(rows, SIDE), at] + both.reshape(2, SIDE, SIDE)
-            ) * inverse[pl.ds(rows, SIDE), pl.ds(col, SIDE)]
-
-        finish(away_at)
-        copies = swap(2, 2 + half, at, SIDE)
-        finish(kept_at)
-        out_ref[zl, :, :, pl.ds(col, SIDE)] = block[2, :, pl.ds(kept_at, SIDE), at]
-        return copies
+        def finish(rows, plane):
+            both = lax.dot_general(
+                turned[pl.ds(rows + ROWS * plane, SIDE), 1536:2048], right, NT,
+                preferred_element_type=jnp.float32)
+            return (block[2, plane, pl.ds(rows, SIDE), at] + both) * inverse[pl.ds(rows, SIDE), pl.ds(col, SIDE)]
+
+        slot = 2 + half
+        pairs = []
+        for plane in range(2):
+            side_out[2, plane, :, at], side_scale_out[slot, plane : plane + 1, 0:SIDE] = encode(
+                finish(away_at, plane))
+            pairs.append((side_out.at[2, plane, :, at], side_in.at[2, plane, :, at]))
+            if plane == 1:
+                pairs.append((side_scale_out.at[slot], side_scale_in.at[slot]))
+                start(pairs, slot)
+            else:
+                start(pairs, slot)
+        for plane in range(2):
+            out_ref[zl, plane, :, pl.ds(col, SIDE)] = finish(kept_at, plane)
+        return [side_copy(source, target, kind, slot) for kind, (source, target) in enumerate(pairs)]
 
     def left_side(n):
         for part in range(2):
@@ -400,7 +416,7 @@
         pltpu.make_async_remote_copy(
             source.at[part], target.at[zl],
             mirror_send.at[kind, n], mirror_recv.at[kind, n], device_id=device, device_id_type=MESH)
-        for n, (part, device) in enumerate(((zl, ring_device(1)), (1 - zl, cross_device(1))))
+        for n, (part, device) in enumerate(((1 - zl, cross_device(1)), (zl, ring_device(1))))
         for kind, (source, target) in enumerate(
             ((mirror_scale_out, mirror_scale_in), (mirror_out, mirror_in)))
     ]
@@ -487,7 +503,7 @@
             dma((CHUNKS,)), dma((CHUNKS, PLANE)), dma((CHUNKS, PLANE)),
             dma((Y,)), dma((Y,)), dma((PLANE,)), dma((PLANE,)),
             dma((len(UP),)), dma((len(UP),)), dma((len(DOWN),)), dma((len(DOWN),)),
-            dma((2, 4)), dma((2, 4)), dma((2, 2)), dma((2, 2)),
+            dma((3, 4)), dma((3, 4)), dma((2, 2)), dma((2, 2)),
         ],
         compiler_params=pltpu.CompilerParams(
             collective_id=0, has_side_effects=True, vmem_limit_bytes=48 << 20),

time: 51.9 us -> 52.1 us (level)
  no operation moved by 1% of the time
where the time goes in v8:
time: 52.1 us; the launch traced here: 51.5 us
  Pallas kernels  49.5 us (95%)
  local copies, waits for them, and re-layouts  1.32 us (3%)
  other arithmetic  0.69 us (1%)
    pallas_call x1, Pallas kernels, stack_up(): pl.pallas_call(kernel, out_shape=jax.ShapeDtypeStruct((2, 2, SIDE, 1024),...  49.5 us
    unnamed x1, local copies, waits for them, and re-layouts  1.32 us

profile of v8, /device:TPU:0, one launch (start us, length us, event | category | flops | bytes accessed | tf_op | source)
XLA Modules:
  0.0 51.5 jit_solution(2076165745498956641)
XLA Ops:
  0.0 0.7 %multiply_bitcast_fusion.flag_ref = s32[4,64]{1,0:T(4,128)S(1)} fusion(s32[64,4]{0,1:T(4,128)} %param.4, s32[64]{0:T(128)} %param.5), kind=kLoop, calls=%fused_computation | loop fusion | flops 256 | bytes 2304 | tf_op jit(solution)/shard_map/mul | solution.py:514
  0.7 49.5 %shard_map.37 = f32[2,2,128,1024]{3,2,1,0:T(8,128)S(1)} custom-call(bf16[64,128,512]{2,1,0:T(8,128)(2,1)} %rec_hbm.1, s32[4,64]{1,0:T(4,128)S(1)} %multiply_bitcast_fusion.flag_ref), custom_call_target="tpu_custom_call" | custom-call | tf_op jit(solution)/shard_map/pallas_call | solution.py:472
  50.2 1.3 %copy.5 = f32[2,2,128,1024]{3,2,1,0:T(8,128)} copy(f32[2,2,128,1024]{3,2,1,0:T(8,128)S(1)} %shard_map.37) | data formatting | bytes 4194304
